TPU v7x, 32 devices: a whole 2x2x4 slice. The times are simulated.
32 devices in a mesh: tile: 8 (over z, y), depth: 4 (over x, core).
Axes of the slice: x: 2, y: 2, z: 4, core: 2. Of those that a mesh axis runs over, the one named last changes fastest.
Arguments:
- positions: float32 [3, 16384], P(None, 'tile'), may hold values from -4 to 4
- log_scales: float32 [3, 16384], P(None, 'tile'), may hold values from -2 to 0
- opacity_logits: float32 [1, 16384], P(None, 'tile'), may hold values from -3 to 1.5
- colors: float32 [3, 16384], P(None, 'tile'), may hold values from 0 to 1
- first_moment: float32 [10, 16384], P(None, 'tile'), may hold values from -3 to 3
- second_moment: float32 [10, 16384], P(None, 'tile'), may hold values from 0.01 to 1
- cameras: float32 [4, 2, 4], replicated, may hold values from -6.4 to 6.4
- background: float32 [3], replicated, may hold values from 0 to 1
- target: float32 [32, 3, 1024], P('tile'), may hold values from 0 to 1
- tile_view: int32 [32], P('tile'), may hold values from 0 to 3
- tile_length: int32 [32], P('tile'), may hold values from 128 to 512
- list_owner: int32 [4, 32, 128, 1], P('depth', 'tile'), may hold values from 0 to 7; in each aligned block of 512 rows (0 to 511, 512 to 1023, ..., all dimensions but the last counted through in order) at most 160 rows name the same one
- list_row: int32 [4, 32, 128], P('depth', 'tile'), may hold values from 0 to 2047
Outputs:
- image: float32 [32, 3, 1024], P('tile')
- new_params: float32 [10, 16384], P(None, 'tile')
- new_first: float32 [10, 16384], P(None, 'tile')
- new_second: float32 [10, 16384], P(None, 'tile')
Inputs may be any that keep to these rules, and one draw needn't show every extreme that they name: `list_owner`: within the entries of one device's block (one depth slab of the tiles of one tile index), no owner is named more than 160 times, a bound that some block reaches.
All inputs are finite; a program needn't handle non-finite values.
Results may differ from a plain program's by a relative error of at most 0.00008.
Values sent between devices are 32-bit elements; how exact they have to be, the bound alone decides.
A program may use at most 64 MiB of HBM per device.

v0:
```python
import functools

import jax
import jax.numpy as jnp
from jax import lax
from jax.experimental import pallas as pl
from jax.experimental.pallas import tpu as pltpu
from jax.sharding import PartitionSpec as P

TILE_SIDE = 32
LANES = 128
MESH = pl.DeviceIdType.MESH
F32 = jnp.float32
BF16 = jnp.bfloat16


def greet(peers):
    barrier = pltpu.get_barrier_semaphore()
    for peer in peers:
        pl.semaphore_signal(barrier, inc=1, device_id=peer, device_id_type=MESH)
    pl.semaphore_wait(barrier, len(peers))


def remote(source, target, send, receive, peer):
    return pltpu.make_async_remote_copy(
        src_ref=source, dst_ref=target, send_sem=send, recv_sem=receive,
        device_id=peer, device_id_type=MESH,
    )


def entry_rows(lists_ref, slot):
    slabs = lists_ref.shape[1]
    owner = jnp.concatenate([lists_ref[slot, d, 0:1, :] for d in range(slabs)], axis=1)
    row = jnp.concatenate([lists_ref[slot, d, 1:2, :] for d in range(slabs)], axis=1)
    return owner, row


def split3(x):
    high = x.astype(BF16)
    rest = x - high.astype(F32)
    middle = rest.astype(BF16)
    low = (rest - middle.astype(F32)).astype(BF16)
    return high, middle, low


def fetch_kernel(
    tiles, depths, owner_ref, row_ref, place_ref, scale_ref, logit_ref, color_ref,
    lists_ref, entry_ref,
    named_ref, param_ref, high_ref, low_ref, answers, got, ask_send, ask_recv, own_sem, send, receive,
):
    lines = param_ref.shape[0]
    highs = lines // 10
    slabs, _, slab = named_ref.shape
    entries = slabs * slab
    for q in range(slabs):
        named_ref[q, 0:1, :] = owner_ref[q]
        named_ref[q, 1:2, :] = row_ref[q : q + 1, :]
    param = 0
    for ref in (place_ref, scale_ref, logit_ref, color_ref):
        for k in range(ref.shape[0]):
            for h in range(highs):
                line = param * highs + h
                param_ref[line : line + 1, :] = ref[k : k + 1, h * LANES : (h + 1) * LANES]
            param += 1
    me_t, me_d = lax.axis_index("tile"), lax.axis_index("depth")
    steps = [(a, b) for a in range(tiles - 1, -1, -1) for b in range(depths) if a or b]

    def to(a, b):
        return {"tile": lax.rem(me_t + a, tiles), "depth": lax.rem(me_d + b, depths)}

    greet([to(a, b) for a, b in steps])
    for a, b in steps:
        remote(
            named_ref.at[lax.rem(me_d + b, depths)], lists_ref.at[me_t, me_d],
            ask_send.at[a, b], ask_recv.at[a, b], to(a, b),
        ).start()
    own = pltpu.make_async_copy(named_ref.at[me_d], lists_ref.at[me_t, me_d], own_sem)
    own.start()
    high, middle, low = split3(param_ref[...])
    high_ref[...] = jnp.concatenate([high, middle], axis=1)
    low_ref[...] = low
    low_iota = lax.broadcasted_iota(jnp.int32, (LANES, entries), 0)
    high_iota = lax.broadcasted_iota(jnp.int32, (highs, entries), 0)

    def asked(a, b):
        return remote(
            named_ref.at[me_d], lists_ref.at[me_t, me_d],
            ask_send.at[a, b], ask_recv.at[a, b], to(a, b),
        )

    def answer(slot):
        owner, row = entry_rows(lists_ref, slot)
        onehot = jnp.where(low_iota == (row & (LANES - 1)), 1.0, 0.0).astype(BF16)
        twice = jnp.concatenate([onehot, onehot], axis=0)
        found = jnp.dot(high_ref[...], twice, preferred_element_type=F32) + jnp.dot(
            low_ref[...], onehot, preferred_element_type=F32
        )
        mask = high_iota == jnp.where(owner == me_t, row >> 7, -1)
        return jnp.concatenate(
            [
                jnp.sum(
                    jnp.where(mask, found[p * highs : (p + 1) * highs], 0.0), axis=0, keepdims=True
                )
                for p in range(10)
            ],
            axis=0,
        )

    def put(ref, step, rows):
        for j in range(slabs):
            ref[step, j * 10 : (j + 1) * 10, :] = rows[:, j * slab : (j + 1) * slab]

    def back(step):
        peer = {"tile": lax.rem(me_t - step + tiles, tiles)}
        return remote(answers.at[step], got.at[step], send.at[step], receive.at[step], peer)

    def serve(step, carry):
        for b in range(depths):
            asked(step, b).wait_recv()
        put(answers, step, answer(lax.rem(me_t - step + tiles, tiles)))
        back(step).start()
        return carry

    lax.fori_loop(1, tiles, serve, 0, unroll=tiles - 1 if tiles <= 8 else 1)
    own.wait()
    for b in range(1, depths):
        asked(0, b).wait_recv()
    put(got, 0, answer(me_t))
    for a, b in steps:
        asked(a, b).wait_send()
    entry_ref[...] = got[0]

    def take(step, carry):
        back(step).wait()
        entry_ref[...] += got[step]
        return carry

    lax.fori_loop(1, tiles, take, 0)


def render_kernel(
    where_ref, view_ref, length_ref, cam_ref, back_ref,
    entry_ref, target_ref,
    image_ref, grad_ref,
    alphas, weights, misses, carries, columns, sums,
):
    slabs = target_ref.shape[1]
    slab = entry_ref.shape[1]
    entries = slabs * slab
    pixels = target_ref.shape[2]
    chunks = pixels // LANES
    groups = entries // 8
    tile = where_ref[0]
    length = length_ref[tile]
    view = view_ref[tile]
    values = [
        jnp.concatenate([entry_ref[j * 10 + p : j * 10 + p + 1, :] for j in range(slabs)], axis=1)
        for p in range(10)
    ]

    first = [cam_ref[view, 0, j] for j in range(4)]
    second = [cam_ref[view, 1, j] for j in range(4)]
    variance = [jnp.exp(2.0 * values[3 + j]) for j in range(3)]
    half = 0.5 * TILE_SIDE
    center_x = first[0] * values[0] + first[1] * values[1] + first[2] * values[2] + first[3] + half
    center_y = second[0] * values[0] + second[1] * values[1] + second[2] * values[2] + second[3] + half
    cov_xx = sum(first[j] * first[j] * variance[j] for j in range(3)) + 0.3
    cov_xy = sum(first[j] * second[j] * variance[j] for j in range(3))
    cov_yy = sum(second[j] * second[j] * variance[j] for j in range(3)) + 0.3
    determinant = cov_xx * cov_yy - cov_xy * cov_xy
    conic_a = cov_yy / determinant
    conic_b = -cov_xy / determinant
    conic_c = cov_xx / determinant
    opacity = 1.0 / (1.0 + jnp.exp(-values[6]))
    place = lax.broadcasted_iota(jnp.int32, (1, entries), 1)
    shown = jnp.where(place < length, opacity, 0.0)
    rows = [center_x, center_y, -0.5 * conic_a, -conic_b, -0.5 * conic_c, shown] + values[7:10]
    table = jnp.concatenate(rows + [jnp.zeros((LANES - len(rows), entries), F32)], axis=0)
    columns[...] = table.T

    lane = lax.broadcasted_iota(jnp.int32, (8, LANES), 1)
    sub = lax.broadcasted_iota(jnp.int32, (8, LANES), 0)
    pixel_x = (lane & (TILE_SIDE - 1)).astype(F32) + 0.5
    pixel_y = (lane >> 5).astype(F32) + 0.5
    rows_chunk = LANES // TILE_SIDE
    ones = jnp.ones((8, LANES), F32)

    def spread(cols, j):
        return jnp.broadcast_to(cols[:, j : j + 1], (8, LANES))

    def forward(g, carry):
        trans, color = carry
        at = pl.ds(pl.multiple_of(g * 8, 8), 8)
        cols = columns[pl.ds(g, 8, stride=groups), :]
        cx, cy, qa, qb, qc, op, red, green, blue = [spread(cols, j) for j in range(9)]
        ex = pixel_x - cx
        ey0 = pixel_y - cy
        qaxx = qa * ex * ex
        qbx = qb * ex
        new_trans, new_color = [], []
        for c in range(chunks):
            ey = ey0 + float(c * rows_chunk)
            alpha = op * jnp.exp(qaxx + (qbx + qc * ey) * ey)
            t = trans[c]
            part = slice(c * LANES, (c + 1) * LANES)
            alphas[at, part] = alpha
            weight = alpha * t
            weights[at, part] = weight
            new_trans.append(t - weight)
            new_color.append(color[3 * c] + weight * red)
            new_color.append(color[3 * c + 1] + weight * green)
            new_color.append(color[3 * c + 2] + weight * blue)
        return new_trans, new_color

    zeros = jnp.zeros((8, LANES), F32)
    trans, color = lax.fori_loop(
        0, groups, forward, ([ones] * chunks, [zeros] * (3 * chunks)), unroll=4
    )

    chosen = lax.broadcasted_iota(jnp.int32, (slabs, LANES), 0) == tile
    behinds = []
    for c in range(chunks):
        part = slice(c * LANES, (c + 1) * LANES)
        run = jnp.where(sub >= 1, pltpu.roll(trans[c], 1, 0), 1.0)
        for s in (1, 2, 4):
            run = run * jnp.where(sub >= s, pltpu.roll(run, s, 0), 1.0)
        carries[:, part] = run
        left = (run * trans[c])[7:8, :]
        total = 0.0
        pulled = zeros
        for k in range(3):
            lit = run * color[3 * c + k]
            shade = jnp.sum(lit, axis=0, keepdims=True) + left * back_ref[k]
            image_ref[k : k + 1, part] = shade
            miss = shade - jnp.sum(
                jnp.where(chosen, target_ref[k, :, part], 0.0), axis=0, keepdims=True
            )
            misses[k, :, part] = jnp.broadcast_to(miss, (8, LANES))
            total = total + miss * shade
            pulled = pulled + miss * lit
        ahead = jnp.where(sub >= 1, pltpu.roll(pulled, 1, 0), 0.0)
        for s in (1, 2, 4):
            ahead = ahead + jnp.where(sub >= s, pltpu.roll(ahead, s, 0), 0.0)
        behinds.append(total - ahead)

    def backward(g, behind):
        at = pl.ds(pl.multiple_of(g * 8, 8), 8)
        spaced = pl.ds(g, 8, stride=groups)
        cols = columns[spaced, :]
        cx, cy, red, green, blue = [spread(cols, j) for j in (0, 1, 6, 7, 8)]
        ex = pixel_x - cx
        ey0 = pixel_y - cy
        new_behind = []
        acc = [zeros] * 6
        for c in range(chunks):
            part = slice(c * LANES, (c + 1) * LANES)
            alpha = alphas[at, part]
            weight = weights[at, part] * carries[:, part]
            m0, m1, m2 = misses[0, :, part], misses[1, :, part], misses[2, :, part]
            pull = m0 * red + m1 * green + m2 * blue
            rest = behind[c] - weight * pull
            new_behind.append(rest)
            grad = weight * pull - rest * (alpha / (1.0 - alpha))
            ey = ey0 + float(c * rows_chunk)
            gy = grad * ey
            acc[0] = acc[0] + grad
            acc[1] = acc[1] + gy
            acc[2] = acc[2] + gy * ey
            acc[3] = acc[3] + weight * m0
            acc[4] = acc[4] + weight * m1
            acc[5] = acc[5] + weight * m2
        gx = acc[0] * ex
        fields = [acc[0], gx, acc[1], gx * ex, acc[1] * ex, acc[2], acc[3], acc[4], acc[5]]
        packed = zeros
        for j, field in enumerate(fields):
            packed = jnp.where(lane == j, jnp.sum(field, axis=1, keepdims=True), packed)
        sums[spaced, :] = packed
        return new_behind

    lax.fori_loop(0, groups, backward, behinds, unroll=4)

    flat = sums[...].T
    s0, sx, sy, sxx, sxy, syy, d_red, d_green, d_blue = [flat[j : j + 1, :] for j in range(9)]
    d_x = conic_a * sx + conic_b * sy
    d_y = conic_b * sx + conic_c * sy
    d_a, d_b, d_c = -0.5 * sxx, -sxy, -0.5 * syy
    d_xx = -(conic_a * conic_a * d_a + conic_a * conic_b * d_b + conic_b * conic_b * d_c)
    d_yy = -(conic_b * conic_b * d_a + conic_b * conic_c * d_b + conic_c * conic_c * d_c)
    d_xy = -(
        2.0 * conic_a * conic_b * d_a
        + (conic_a * conic_c + conic_b * conic_b) * d_b
        + 2.0 * conic_b * conic_c * d_c
    )
    out = [first[j] * d_x + second[j] * d_y for j in range(3)]
    for j in range(3):
        d_var = first[j] * first[j] * d_xx + first[j] * second[j] * d_xy + second[j] * second[j] * d_yy
        out.append(2.0 * variance[j] * d_var)
    out += [s0 * (1.0 - opacity), d_red, d_green, d_blue]
    out = jnp.concatenate(out, axis=0)
    for j in range(slabs):
        grad_ref[j * 10 : (j + 1) * 10, :] = out[:, j * slab : (j + 1) * slab]


def collect_kernel(
    tiles, depths, own_ref, image_ref, lists_ref, gradient_ref, picture_ref,
    images_ref, out_ref, inbox, partial, pieces, mine,
    send, receive, image_send, image_recv, image_own, cut_send, cut_recv, all_send, all_recv,
):
    lines = out_ref.shape[0]
    highs = lines // 10
    quarter = lines // depths
    slabs, slab = lists_ref.shape[1], lists_ref.shape[3]
    entries = slabs * slab
    me_t, me_d = lax.axis_index("tile"), lax.axis_index("depth")

    def along(step):
        return {"depth": lax.rem(me_d + step, depths)}

    def across(step):
        return {"tile": lax.rem(me_t + step, tiles)}

    def grads(step):
        return remote(own_ref, inbox.at[step], send.at[step], receive.at[step], across(step))

    greet([across(s) for s in range(1, tiles)] + [along(s) for s in range(1, depths)])
    for step in range(tiles - 1, 0, -1):
        grads(step).start()
    image_copies = [
        remote(image_ref, images_ref.at[me_d], image_send.at[s], image_recv.at[s], along(s))
        for s in range(1, depths)
    ]
    image_copies.append(pltpu.make_async_copy(image_ref, images_ref.at[me_d], image_own))
    for copy in image_copies:
        copy.start()

    high_iota = lax.broadcasted_iota(jnp.int32, (highs, entries), 0)
    low_iota = lax.broadcasted_iota(jnp.int32, (LANES, entries), 0)

    def placed(block, slot):
        owner, row = entry_rows(lists_ref, slot)
        onehot = jnp.where(low_iota == (row & (LANES - 1)), 1.0, 0.0).astype(BF16)
        mask = high_iota == jnp.where(owner == me_t, row >> 7, -1)
        wide = jnp.concatenate([block[j * 10 : (j + 1) * 10, :] for j in range(slabs)], axis=1)
        spots = jnp.concatenate(
            [jnp.where(mask, wide[p : p + 1, :], 0.0) for p in range(10)], axis=0
        )
        high = spots.astype(BF16)
        middle = (spots - high.astype(F32)).astype(BF16)
        dims = (((1,), (1,)), ((), ()))
        return lax.dot_general(
            high, onehot, dims, preferred_element_type=F32
        ) + lax.dot_general(middle, onehot, dims, preferred_element_type=F32)

    partial[...] = placed(own_ref[...], me_t)

    def add(step, carry):
        grads(step).wait()
        partial[...] += placed(inbox[step], lax.rem(me_t - step + tiles, tiles))
        return carry

    lax.fori_loop(1, tiles, add, 0, unroll=tiles - 1 if tiles <= 8 else 1)
    for copy in image_copies:
        copy.wait()

    def rows_of(index):
        return pl.ds(pl.multiple_of(index * quarter, 8), quarter)

    cuts = [
        remote(
            partial.at[rows_of(lax.rem(me_d + s, depths))], pieces.at[s],
            cut_send.at[s], cut_recv.at[s], along(s),
        )
        for s in range(1, depths)
    ]
    for copy in cuts:
        copy.start()
    total = partial[rows_of(me_d), :]
    for s, copy in enumerate(cuts):
        copy.wait()
        total = total + pieces[s + 1]
    mine[...] = total
    shares = [
        remote(mine, out_ref.at[rows_of(me_d)], all_send.at[s], all_recv.at[s], along(s))
        for s in range(1, depths)
    ]
    for copy in shares:
        copy.start()
    out_ref[rows_of(me_d), :] = total
    for d in range(depths):
        for k in range(3):
            picture_ref[k, d : d + 1, :] = images_ref[d, k : k + 1, :]
    for copy in shares:
        copy.wait()
    for p in range(10):
        for h in range(highs):
            line = p * highs + h
            gradient_ref[p : p + 1, h * LANES : (h + 1) * LANES] = out_ref[line : line + 1, :]


def adam_update(param, first, second, gradient):
    new_first = 0.9 * first + 0.1 * gradient
    new_second = 0.999 * second + 0.001 * gradient * gradient
    corrected = new_first / (1.0 - 0.9**10) / (jnp.sqrt(new_second / (1.0 - 0.999**10)) + 1e-08)
    return (param - 0.05 * corrected, new_first, new_second)


def body(
    positions, log_scales, opacity_logits, colors, first_moment, second_moment,
    cameras, background, target, tile_view, tile_length, list_owner, list_row,
):
    tiles_here, _, pixels = target.shape
    slab = list_row.shape[2]
    depth_count = lax.axis_size("depth")
    entries = slab * depth_count
    here = lax.axis_index("depth").astype(jnp.int32).reshape(1)
    assert tiles_here == depth_count
    params = jnp.concatenate([positions, log_scales, opacity_logits, colors], axis=0)
    splats = params.shape[1]
    lines = 10 * splats // LANES
    tile_count = lax.axis_size("tile")
    assert 10 * slab * depth_count % LANES == 0 and slab == LANES
    smem = pl.BlockSpec(memory_space=pltpu.SMEM)
    vmem = pl.BlockSpec(memory_space=pltpu.VMEM)
    dma = pltpu.SemaphoreType.DMA
    block = (10 * depth_count, slab)
    limit = 60 << 20
    lists, entry = pl.pallas_call(
        functools.partial(fetch_kernel, tile_count, depth_count),
        out_shape=[
            jax.ShapeDtypeStruct((tile_count, depth_count, 2, slab), jnp.int32),
            jax.ShapeDtypeStruct(block, F32),
        ],
        in_specs=[vmem] * 6,
        out_specs=[vmem] * 2,
        scratch_shapes=[
            pltpu.VMEM((depth_count, 2, slab), jnp.int32),
            pltpu.VMEM((lines, LANES), F32),
            pltpu.VMEM((lines, 2 * LANES), BF16),
            pltpu.VMEM((lines, LANES), BF16),
            pltpu.VMEM((tile_count,) + block, F32),
            pltpu.VMEM((tile_count,) + block, F32),
            dma((tile_count, depth_count)),
            dma((tile_count, depth_count)),
            dma,
            dma((tile_count,)),
            dma((tile_count,)),
        ],
        name="fetch",
        compiler_params=pltpu.CompilerParams(
            collective_id=1, has_side_effects=True, vmem_limit_bytes=limit
        ),
    )(
        list_owner.reshape(tiles_here, 1, slab), list_row[0],
        positions, log_scales, opacity_logits, colors,
    )
    own_image, own_grad = pl.pallas_call(
        render_kernel,
        out_shape=[
            jax.ShapeDtypeStruct((3, pixels), F32),
            jax.ShapeDtypeStruct(block, F32),
        ],
        in_specs=[smem] * 5 + [vmem] * 2,
        out_specs=[vmem] * 2,
        scratch_shapes=[
            pltpu.VMEM((entries, pixels), F32),
            pltpu.VMEM((entries, pixels), F32),
            pltpu.VMEM((3, 8, pixels), F32),
            pltpu.VMEM((8, pixels), F32),
            pltpu.VMEM((entries, LANES), F32),
            pltpu.VMEM((entries, LANES), F32),
        ],
        name="render",
        compiler_params=pltpu.CompilerParams(vmem_limit_bytes=limit),
    )(here, tile_view, tile_length, cameras, background, entry, target.transpose(1, 0, 2))
    quarter = lines // depth_count
    gradient, picture = pl.pallas_call(
        functools.partial(collect_kernel, tile_count, depth_count),
        out_shape=[
            jax.ShapeDtypeStruct((10, splats), F32),
            jax.ShapeDtypeStruct((3, depth_count, pixels), F32),
        ],
        in_specs=[vmem] * 3,
        out_specs=[vmem] * 2,
        scratch_shapes=[
            pltpu.VMEM((depth_count, 3, pixels), F32),
            pltpu.VMEM((lines, LANES), F32),
            pltpu.VMEM((tile_count,) + block, F32),
            pltpu.VMEM((lines, LANES), F32),
            pltpu.VMEM((depth_count, quarter, LANES), F32),
            pltpu.VMEM((quarter, LANES), F32),
            dma((tile_count,)),
            dma((tile_count,)),
            dma((depth_count,)),
            dma((depth_count,)),
            dma,
            dma((depth_count,)),
            dma((depth_count,)),
            dma((depth_count,)),
            dma((depth_count,)),
        ],
        name="collect",
        compiler_params=pltpu.CompilerParams(
            collective_id=2, has_side_effects=True, vmem_limit_bytes=limit
        ),
    )(own_grad, own_image, lists)
    image = picture.transpose(1, 0, 2)
    new_params, new_first, new_second = adam_update(params, first_moment, second_moment, gradient)
    return (image, new_params, new_first, new_second)


def solution(mesh):
    placed = (
        P(None, "tile"),
        P(None, "tile"),
        P(None, "tile"),
        P(None, "tile"),
        P(None, "tile"),
        P(None, "tile"),
        P(),
        P(),
        P("tile", None, None),
        P("tile"),
        P("tile"),
        P("depth", "tile", None, None),
        P("depth", "tile", None),
    )
    return jax.shard_map(
        body,
        mesh=mesh,
        in_specs=placed,
        out_specs=(P("tile", None, None), P(None, "tile"), P(None, "tile"), P(None, "tile")),
        check_vma=False,
    )
```

profile of v0, /device:TPU:0, one launch (start us, length us, event | category | flops | bytes accessed | tf_op | source)
XLA Modules:
  0.0 46.9 jit_solution(10150077368214545945)
XLA Ops:
  0.6 0.0 copy-start.3
  0.6 18.3 %fetch.1 = (s32[8,4,2,128]{3,2,1,0:T(2,128)}, f32[40,128]{1,0:T(8,128)}) custom-call(s32[4,1,128]{2,1,0:T(1,128)} %bitcast.7, s32[4,128]{1,0:T(4,128)} %bitcast.8, f32[3,2048]{1,0:T(4,128)} %place_ref.1, f32[3,2048]{1,0:T(4,128)} %scale_ref.1, f32[1,2048]{1,0:T(1,128)} %logit_ref.1, f32[3,2048]{1,0:T(4,128)} %color_ref.1), custom_call_target="tpu_custom_call" | custom-call | tf_op jit(solution)/shard_map/fetch/pallas_call | solution.py:427
  18.9 0.0 copy-start.2
  18.9 8.6 %render.1 = (f32[3,1024]{1,0:T(4,128)}, f32[40,128]{1,0:T(8,128)}) custom-call(s32[1]{0:T(128)} %bitcast.where_ref, s32[4]{0:T(128)} %view_ref.1, s32[4]{0:T(128)} %length_ref.1, f32[4,2,4]{2,1,0:T(2,128)} %cam_ref.1, f32[3]{0:T(128)} %back_ref.1, f32[40,128]{1,0:T(8,128)} %get-tuple-element.10.entry_ref, f32[3,4,1024]{2,1,0:T(4,128)} %bitcast.5), custom_call_target="tpu_custom_call" | custom-call | tf_op jit(solution)/shard_map/render/pallas_call | solution.py:456
  27.6 0.0 copy-start
  27.6 0.0 copy-start.1
  27.6 0.0 copy-start.5
  27.6 16.9 %collect.1 = (f32[10,2048]{1,0:T(8,128)}, f32[3,4,1024]{2,1,0:T(4,128)}) custom-call(f32[40,128]{1,0:T(8,128)} %get-tuple-element.11.own_ref, f32[3,1024]{1,0:T(4,128)} %get-tuple-element.12.image_ref, s32[8,4,2,128]{3,2,1,0:T(2,128)} %get-tuple-element.13.lists_ref), custom_call_target="tpu_custom_call" | custom-call | tf_op jit(solution)/shard_map/collect/pallas_call | solution.py:476
  44.5 0.0 copy-done.3
  44.5 0.0 copy-done.2
  44.5 0.0 copy-done
  44.5 0.0 copy-done.1
  44.5 0.0 copy-done.5
  44.5 0.0 copy-start.4
  44.5 1.8 %maximum_subtract_fusion = (f32[10,2048]{1,0:T(8,128)}, f32[10,2048]{1,0:T(8,128)}, f32[10,2048]{1,0:T(8,128)}) fusion(f32[3,2048]{1,0:T(4,128)S(1)} %copy-done.2, f32[1,2048]{1,0:T(1,128)S(1)} %copy-done.5, f32[3,2048]{1,0:T(4,128)S(1)} %copy-done.1, f32[3,2048]{1,0:T(4,128)S(1)} %copy-done, f32[10,2048]{1,0:T(8,128)} %get-tuple-element.15, ...), kind=kLoop, calls=%fused_computation.2 | loop fusion | flops 327680 | bytes 573440 | tf_op jit(solution)/shard_map/sub | solution.py:404
  46.3 0.0 copy-done.4
  46.3 0.6 %copy.18 = f32[4,3,1024]{2,0,1:T(4,128)} copy(f32[4,3,1024]{2,0,1:T(4,128)S(1)} %bitcast.6) | data formatting | bytes 98304
Async XLA Ops:
  0.6 43.8 %copy-start.3 = (f32[10,2048]{1,0:T(8,128)S(1)}, f32[10,2048]{1,0:T(8,128)}, u32[]{:S(2)}) copy-start(f32[10,2048]{1,0:T(8,128)} %param.17) | copy-start | bytes 245764
  18.9 25.5 %copy-start.2 = (f32[3,2048]{1,0:T(4,128)S(1)}, f32[3,2048]{1,0:T(4,128)}, u32[]{:S(2)}) copy-start(f32[3,2048]{1,0:T(4,128)} %color_ref.1) | copy-start | bytes 73732
  27.6 16.9 %copy-start = (f32[3,2048]{1,0:T(4,128)S(1)}, f32[3,2048]{1,0:T(4,128)}, u32[]{:S(2)}) copy-start(f32[3,2048]{1,0:T(4,128)} %place_ref.1) | copy-start | bytes 73732
  27.6 16.9 %copy-start.1 = (f32[3,2048]{1,0:T(4,128)S(1)}, f32[3,2048]{1,0:T(4,128)}, u32[]{:S(2)}) copy-start(f32[3,2048]{1,0:T(4,128)} %scale_ref.1) | copy-start | bytes 73732
  27.6 16.9 %copy-start.5 = (f32[1,2048]{1,0:T(1,128)S(1)}, f32[1,2048]{1,0:T(1,128)}, u32[]{:S(2)}) copy-start(f32[1,2048]{1,0:T(1,128)} %logit_ref.1) | copy-start | bytes 24580
  44.5 1.8 %copy-start.4 = (f32[3,4,1024]{2,1,0:T(4,128)S(1)}, f32[3,4,1024]{2,1,0:T(4,128)}, u32[]{:S(2)}) copy-start(f32[3,4,1024]{2,1,0:T(4,128)} %get-tuple-element.14) | copy-start | bytes 147460
where the time goes:
time: 47.2 us; the launch traced here: 46.9 us
  Pallas kernels  43.8 us (93%)
  other arithmetic  1.81 us (4%)
  between operations  0.72 us (2%)
  local copies, waits for them, and re-layouts  0.65 us (1%)
    pallas_call x1, Pallas kernels, body(): pl.pallas_call(functools.partial(fetch_kernel, tile_count, depth_count),...  18.3 us
    pallas_call x1, Pallas kernels, body(): pl.pallas_call(functools.partial(collect_kernel, tile_count, depth_count)...  16.9 us
    pallas_call x1, Pallas kernels, body(): pl.pallas_call(render_kernel, out_shape=[jax.ShapeDtypeStruct((3, pixels)...  8.64 us
    sub x1, other arithmetic, adam_update(): return (param - 0.05 * corrected, new_first, new_second)  1.81 us

commit v1 on v0

v1 whole, which is shorter than its diff:
```python
import functools

import jax
import jax.numpy as jnp
from jax import lax
from jax.experimental import pallas as pl
from jax.experimental.pallas import tpu as pltpu
from jax.sharding import PartitionSpec as P

TILE_SIDE = 32
LANES = 128
MESH = pl.DeviceIdType.MESH
F32 = jnp.float32
BF16 = jnp.bfloat16


def greet(peers):
    barrier = pltpu.get_barrier_semaphore()
    for peer in peers:
        pl.semaphore_signal(barrier, inc=1, device_id=peer, device_id_type=MESH)
    pl.semaphore_wait(barrier, len(peers))


def remote(source, target, send, receive, peer):
    return pltpu.make_async_remote_copy(
        src_ref=source, dst_ref=target, send_sem=send, recv_sem=receive,
        device_id=peer, device_id_type=MESH,
    )


def split3(x):
    high = x.astype(BF16)
    rest = x - high.astype(F32)
    middle = rest.astype(BF16)
    low = (rest - middle.astype(F32)).astype(BF16)
    return high, middle, low


def flip(index, step, size):
    out, bit = 0, 1
    while bit < size:
        mine = lax.rem(lax.div(index, bit), 2)
        if isinstance(step, int):
            out = out + bit * (1 - mine if (step // bit) % 2 else mine)
        else:
            out = out + bit * lax.rem(mine + lax.rem(lax.div(step, bit), 2), 2)
        bit *= 2
    return out


def step_kernel(
    tiles, depths,
    owner_in, row_in, place_in, scale_in, logit_in, color_in, first_in, second_in,
    target_in, view_in, length_in, cam_in, back_in,
    picture_ref, new_param_ref, new_first_ref, new_second_ref,
    owner_ref, row_ref, place_ref, scale_ref, logit_ref, color_ref, first_ref, second_ref,
    target_ref, view_ref, length_ref, cam_ref, back_ref, loads,
    named_ref, lists_ref, param_ref, high_ref, low_ref, answers, got,
    ask_send, ask_recv, send, receive,
    alphas, weights, misses, carries, columns, sums, grad_ref, image_ref, images_ref,
    inbox, partial, half_in, half_sum, pieces, whole_out,
    grad_send, grad_recv, image_send, image_recv, pair_send, pair_recv, cut_send, cut_recv,
    all_send, all_recv,
):
    lines = param_ref.shape[0]
    highs = lines // 10
    slabs, _, slab = named_ref.shape
    entries = slabs * slab
    pixels = target_ref.shape[2]
    splats = highs * LANES
    me_t, me_d = lax.axis_index("tile"), lax.axis_index("depth")
    small = tiles <= 8
    depth_of = [me_d] + [flip(me_d, b, depths) for b in range(1, depths)]
    tile_of = [me_t] + [flip(me_t, a, tiles) for a in range(1, tiles)] if small else None
    steps = [(a, b) for a in range(tiles - 1, -1, -1) for b in range(depths) if a or b]

    def tile_at(step):
        return tile_of[step] if small else flip(me_t, step, tiles)

    def to(a, b):
        return {"tile": tile_at(a), "depth": depth_of[b]}

    def across(step):
        return {"tile": tile_at(step)}

    def along(step):
        return {"depth": depth_of[step]}

    def each_tile(function):
        if small:
            for step in range(1, tiles):
                function(step)
        else:
            def one(step, carry):
                function(step)
                return carry

            lax.fori_loop(1, tiles, one, 0)

    barrier = pltpu.get_barrier_semaphore()
    for a, b in steps:
        pl.semaphore_signal(barrier, inc=1, device_id=to(a, b), device_id_type=MESH)
    pairs = [
        (owner_in, owner_ref), (row_in, row_ref), (place_in, place_ref), (scale_in, scale_ref),
        (logit_in, logit_ref), (color_in, color_ref), (view_in, view_ref), (length_in, length_ref),
        (cam_in, cam_ref), (back_in, back_ref), (target_in, target_ref),
        (first_in, first_ref), (second_in, second_ref),
    ]
    copies = [
        pltpu.make_async_copy(source, target, loads.at[i])
        for i, (source, target) in enumerate(pairs)
    ]
    for copy in copies:
        copy.start()
    for copy in copies[:2]:
        copy.wait()
    for q in range(slabs):
        named_ref[q] = owner_ref[q] * splats + row_ref[q : q + 1, :]
    pl.semaphore_wait(barrier, len(steps))

    def asked(a, b):
        return remote(
            named_ref.at[depth_of[b]], lists_ref.at[me_t, me_d],
            ask_send.at[a, b], ask_recv.at[a, b], to(a, b),
        )

    for a, b in steps:
        asked(a, b).start()
    lists_ref[me_t, me_d] = named_ref[me_d]
    for copy in copies[2:6]:
        copy.wait()
    param = 0
    for ref in (place_ref, scale_ref, logit_ref, color_ref):
        for k in range(ref.shape[0]):
            for h in range(highs):
                line = param * highs + h
                param_ref[line : line + 1, :] = ref[k : k + 1, h * LANES : (h + 1) * LANES]
            param += 1
    high, middle, low = split3(param_ref[...])
    high_ref[...] = jnp.concatenate([high, middle], axis=1)
    low_ref[...] = low
    low_iota = lax.broadcasted_iota(jnp.int32, (LANES, entries), 0)
    high_iota = lax.broadcasted_iota(jnp.int32, (highs, entries), 0) + me_t * highs

    def entry_names(slot):
        names = jnp.concatenate([lists_ref[slot, d] for d in range(slabs)], axis=1)
        onehot = jnp.where(low_iota == (names & (LANES - 1)), 1.0, 0.0).astype(BF16)
        return onehot, high_iota == (names >> 7)

    def answer(slot):
        onehot, mask = entry_names(slot)
        twice = jnp.concatenate([onehot, onehot], axis=0)
        found = jnp.dot(high_ref[...], twice, preferred_element_type=F32) + jnp.dot(
            low_ref[...], onehot, preferred_element_type=F32
        )
        return jnp.concatenate(
            [
                jnp.sum(
                    jnp.where(mask, found[p * highs : (p + 1) * highs], 0.0), axis=0, keepdims=True
                )
                for p in range(10)
            ],
            axis=0,
        )

    def put(ref, step, rows):
        for j in range(slabs):
            ref[step, j * 10 : (j + 1) * 10, :] = rows[:, j * slab : (j + 1) * slab]

    def back(step):
        return remote(
            answers.at[step], got.at[step], send.at[step], receive.at[step], across(step)
        )

    def serve(step):
        for b in range(depths):
            asked(step, b).wait_recv()
        put(answers, step, answer(tile_at(step)))
        back(step).start()

    each_tile(serve)
    for b in range(1, depths):
        asked(0, b).wait_recv()
    put(got, 0, answer(me_t))
    for a, b in steps:
        asked(a, b).wait_send()
    for copy in copies[6:]:
        copy.wait()

    def take(step):
        back(step).wait()
        got[0] += got[step]

    each_tile(take)
    found = got[0]

    chunks = pixels // LANES
    groups = entries // 8
    length = length_ref[me_d]
    view = view_ref[me_d]
    values = [
        jnp.concatenate([found[j * 10 + p : j * 10 + p + 1, :] for j in range(slabs)], axis=1)
        for p in range(10)
    ]

    first = [cam_ref[view, 0, j] for j in range(4)]
    second = [cam_ref[view, 1, j] for j in range(4)]
    variance = [jnp.exp(2.0 * values[3 + j]) for j in range(3)]
    half = 0.5 * TILE_SIDE
    center_x = first[0] * values[0] + first[1] * values[1] + first[2] * values[2] + first[3] + half
    center_y = second[0] * values[0] + second[1] * values[1] + second[2] * values[2] + second[3] + half
    cov_xx = sum(first[j] * first[j] * variance[j] for j in range(3)) + 0.3
    cov_xy = sum(first[j] * second[j] * variance[j] for j in range(3))
    cov_yy = sum(second[j] * second[j] * variance[j] for j in range(3)) + 0.3
    determinant = cov_xx * cov_yy - cov_xy * cov_xy
    conic_a = cov_yy / determinant
    conic_b = -cov_xy / determinant
    conic_c = cov_xx / determinant
    opacity = 1.0 / (1.0 + jnp.exp(-values[6]))
    place = lax.broadcasted_iota(jnp.int32, (1, entries), 1)
    shown = jnp.where(place < length, opacity, 0.0)
    rows = [center_x, center_y, -0.5 * conic_a, -conic_b, -0.5 * conic_c, shown] + values[7:10]
    table = jnp.concatenate(rows + [jnp.zeros((LANES - len(rows), entries), F32)], axis=0)
    columns[...] = table.T

    lane = lax.broadcasted_iota(jnp.int32, (8, LANES), 1)
    sub = lax.broadcasted_iota(jnp.int32, (8, LANES), 0)
    pixel_x = (lane & (TILE_SIDE - 1)).astype(F32) + 0.5
    pixel_y = (lane >> 5).astype(F32) + 0.5
    rows_chunk = LANES // TILE_SIDE
    ones = jnp.ones((8, LANES), F32)

    def spread(cols, j):
        return jnp.broadcast_to(cols[:, j : j + 1], (8, LANES))

    def forward(g, carry):
        trans, color = carry
        at = pl.ds(pl.multiple_of(g * 8, 8), 8)
        cols = columns[pl.ds(g, 8, stride=groups), :]
        cx, cy, qa, qb, qc, op, red, green, blue = [spread(cols, j) for j in range(9)]
        ex = pixel_x - cx
        ey0 = pixel_y - cy
        qaxx = qa * ex * ex
        qbx = qb * ex
        new_trans, new_color = [], []
        for c in range(chunks):
            ey = ey0 + float(c * rows_chunk)
            alpha = op * jnp.exp(qaxx + (qbx + qc * ey) * ey)
            t = trans[c]
            part = slice(c * LANES, (c + 1) * LANES)
            alphas[at, part] = alpha
            weight = alpha * t
            weights[at, part] = weight
            new_trans.append(t - weight)
            new_color.append(color[3 * c] + weight * red)
            new_color.append(color[3 * c + 1] + weight * green)
            new_color.append(color[3 * c + 2] + weight * blue)
        return new_trans, new_color

    zeros = jnp.zeros((8, LANES), F32)
    trans, color = lax.fori_loop(
        0, groups, forward, ([ones] * chunks, [zeros] * (3 * chunks)), unroll=4
    )

    chosen = lax.broadcasted_iota(jnp.int32, (slabs, LANES), 0) == me_d
    behinds = []
    for c in range(chunks):
        part = slice(c * LANES, (c + 1) * LANES)
        run = jnp.where(sub >= 1, pltpu.roll(trans[c], 1, 0), 1.0)
        for s in (1, 2, 4):
            run = run * jnp.where(sub >= s, pltpu.roll(run, s, 0), 1.0)
        carries[:, part] = run
        left = (run * trans[c])[7:8, :]
        total = 0.0
        pulled = zeros
        for k in range(3):
            lit = run * color[3 * c + k]
            shade = jnp.sum(lit, axis=0, keepdims=True) + left * back_ref[k]
            image_ref[k : k + 1, part] = shade
            miss = shade - jnp.sum(
                jnp.where(chosen, target_ref[k, :, part], 0.0), axis=0, keepdims=True
            )
            misses[k, :, part] = jnp.broadcast_to(miss, (8, LANES))
            total = total + miss * shade
            pulled = pulled + miss * lit
        ahead = jnp.where(sub >= 1, pltpu.roll(pulled, 1, 0), 0.0)
        for s in (1, 2, 4):
            ahead = ahead + jnp.where(sub >= s, pltpu.roll(ahead, s, 0), 0.0)
        behinds.append(total - ahead)

    images_ref[me_d] = image_ref[...]
    image_copies = [
        remote(image_ref, images_ref.at[me_d], image_send.at[s], image_recv.at[s], along(s))
        for s in range(1, depths)
    ]
    for copy in image_copies:
        copy.start()

    def backward(g, behind):
        at = pl.ds(pl.multiple_of(g * 8, 8), 8)
        spaced = pl.ds(g, 8, stride=groups)
        cols = columns[spaced, :]
        cx, cy, red, green, blue = [spread(cols, j) for j in (0, 1, 6, 7, 8)]
        ex = pixel_x - cx
        ey0 = pixel_y - cy
        new_behind = []
        acc = [zeros] * 6
        for c in range(chunks):
            part = slice(c * LANES, (c + 1) * LANES)
            alpha = alphas[at, part]
            weight = weights[at, part] * carries[:, part]
            m0, m1, m2 = misses[0, :, part], misses[1, :, part], misses[2, :, part]
            pull = m0 * red + m1 * green + m2 * blue
            rest = behind[c] - weight * pull
            new_behind.append(rest)
            grad = weight * pull - rest * (alpha / (1.0 - alpha))
            ey = ey0 + float(c * rows_chunk)
            gy = grad * ey
            acc[0] = acc[0] + grad
            acc[1] = acc[1] + gy
            acc[2] = acc[2] + gy * ey
            acc[3] = acc[3] + weight * m0
            acc[4] = acc[4] + weight * m1
            acc[5] = acc[5] + weight * m2
        gx = acc[0] * ex
        fields = [acc[0], gx, acc[1], gx * ex, acc[1] * ex, acc[2], acc[3], acc[4], acc[5]]
        packed = zeros
        for j, field in enumerate(fields):
            packed = jnp.where(lane == j, jnp.sum(field, axis=1, keepdims=True), packed)
        sums[spaced, :] = packed
        return new_behind

    lax.fori_loop(0, groups, backward, behinds, unroll=4)

    flat = sums[...].T
    s0, sx, sy, sxx, sxy, syy, d_red, d_green, d_blue = [flat[j : j + 1, :] for j in range(9)]
    d_x = conic_a * sx + conic_b * sy
    d_y = conic_b * sx + conic_c * sy
    d_a, d_b, d_c = -0.5 * sxx, -sxy, -0.5 * syy
    d_xx = -(conic_a * conic_a * d_a + conic_a * conic_b * d_b + conic_b * conic_b * d_c)
    d_yy = -(conic_b * conic_b * d_a + conic_b * conic_c * d_b + conic_c * conic_c * d_c)
    d_xy = -(
        2.0 * conic_a * conic_b * d_a
        + (conic_a * conic_c + conic_b * conic_b) * d_b
        + 2.0 * conic_b * conic_c * d_c
    )
    out = [first[j] * d_x + second[j] * d_y for j in range(3)]
    for j in range(3):
        d_var = first[j] * first[j] * d_xx + first[j] * second[j] * d_xy + second[j] * second[j] * d_yy
        out.append(2.0 * variance[j] * d_var)
    out += [s0 * (1.0 - opacity), d_red, d_green, d_blue]
    out = jnp.concatenate(out, axis=0)
    for j in range(slabs):
        grad_ref[j * 10 : (j + 1) * 10, :] = out[:, j * slab : (j + 1) * slab]

    def grads(step):
        return remote(
            grad_ref, inbox.at[step], grad_send.at[step], grad_recv.at[step], across(step)
        )

    for step in range(tiles - 1, 0, -1):
        grads(step).start()

    def placed(block, slot):
        onehot, mask = entry_names(slot)
        wide = jnp.concatenate([block[j * 10 : (j + 1) * 10, :] for j in range(slabs)], axis=1)
        spots = jnp.concatenate(
            [jnp.where(mask, wide[p : p + 1, :], 0.0) for p in range(10)], axis=0
        )
        high = spots.astype(BF16)
        middle = (spots - high.astype(F32)).astype(BF16)
        dims = (((1,), (1,)), ((), ()))
        return lax.dot_general(
            high, onehot, dims, preferred_element_type=F32
        ) + lax.dot_general(middle, onehot, dims, preferred_element_type=F32)

    partial[...] = placed(grad_ref[...], me_t)

    def add(step):
        grads(step).wait()
        partial[...] += placed(inbox[step], tile_at(step))

    each_tile(add)

    size = lines // 2

    def side(index):
        return pl.ds(pl.multiple_of(index * size, 8), size)

    core = lax.rem(me_d, 2)
    mine, other = side(core), side(1 - core)
    pair = remote(partial.at[other], half_in, pair_send.at[0], pair_recv.at[0], along(1))
    pair.start()
    pair.wait()
    half_sum[...] = partial[mine, :] + half_in[...]
    cuts = [
        remote(half_sum, pieces.at[s], cut_send.at[s], cut_recv.at[s], along(s))
        for s in range(2, depths, 2)
    ]
    for copy in cuts:
        copy.start()
    total = half_sum[...]
    for copy in cuts:
        copy.wait_recv()
    for s in range(2, depths, 2):
        total = total + pieces[s]
    whole_out[mine, :] = total
    share = remote(
        whole_out.at[mine], whole_out.at[mine], pair_send.at[1], pair_recv.at[1], along(1)
    )
    share.start()
    for copy in cuts:
        copy.wait_send()
    for copy in image_copies:
        copy.wait()
    for d in range(depths):
        for k in range(3):
            picture_ref[k, d : d + 1, :] = images_ref[d, k : k + 1, :]
    share.wait()
    for h in range(highs):
        part = slice(h * LANES, (h + 1) * LANES)
        spaced = pl.ds(h, 10, stride=highs)
        new_param_ref[:, part], new_first_ref[:, part], new_second_ref[:, part] = adam_update(
            param_ref[spaced, :], first_ref[:, part], second_ref[:, part], whole_out[spaced, :]
        )


def adam_update(param, first, second, gradient):
    new_first = 0.9 * first + 0.1 * gradient
    new_second = 0.999 * second + 0.001 * gradient * gradient
    corrected = new_first / (1.0 - 0.9**10) / (jnp.sqrt(new_second / (1.0 - 0.999**10)) + 1e-08)
    return (param - 0.05 * corrected, new_first, new_second)


def finish_kernel(*refs):
    count = (len(refs) - 1) // 2
    copies = [
        pltpu.make_async_copy(refs[i], refs[count + i], refs[-1].at[i]) for i in range(count)
    ]
    for copy in copies:
        copy.start()
    for copy in copies:
        copy.wait()


def body(
    positions, log_scales, opacity_logits, colors, first_moment, second_moment,
    cameras, background, target, tile_view, tile_length, list_owner, list_row,
):
    tiles_here, _, pixels = target.shape
    slab = list_row.shape[2]
    depths = lax.axis_size("depth")
    tiles = lax.axis_size("tile")
    entries = slab * depths
    splats = positions.shape[1]
    lines = 10 * splats // LANES
    assert tiles_here == depths and slab == LANES and depths % 2 == 0
    assert tiles & (tiles - 1) == 0 and depths & (depths - 1) == 0
    dma = pltpu.SemaphoreType.DMA
    block = (10 * depths, slab)
    limit = 60 << 20
    args = [
        list_owner.reshape(tiles_here, 1, slab), list_row[0],
        positions, log_scales, opacity_logits, colors, first_moment, second_moment,
        target.transpose(1, 0, 2), tile_view, tile_length, cameras, background,
    ]
    held = [
        (pltpu.VMEM if i < 9 else pltpu.SMEM)(arg.shape, arg.dtype) for i, arg in enumerate(args)
    ]
    results = [(3, tiles_here, pixels)] + [(10, splats)] * 3
    done = pl.pallas_call(
        functools.partial(step_kernel, tiles, depths),
        out_shape=[pltpu.VMEM(shape, F32) for shape in results],
        in_specs=[pl.BlockSpec(memory_space=pl.ANY)] * len(args),
        out_specs=[pl.BlockSpec(memory_space=pltpu.VMEM)] * len(results),
        scratch_shapes=held + [
            dma((len(args),)),
            pltpu.VMEM((depths, 1, slab), jnp.int32),
            pltpu.VMEM((tiles, depths, 1, slab), jnp.int32),
            pltpu.VMEM((lines, LANES), F32),
            pltpu.VMEM((lines, 2 * LANES), BF16),
            pltpu.VMEM((lines, LANES), BF16),
            pltpu.VMEM((tiles,) + block, F32),
            pltpu.VMEM((tiles,) + block, F32),
            dma((tiles, depths)),
            dma((tiles, depths)),
            dma((tiles,)),
            dma((tiles,)),
            pltpu.VMEM((entries, pixels), F32),
            pltpu.VMEM((entries, pixels), F32),
            pltpu.VMEM((3, 8, pixels), F32),
            pltpu.VMEM((8, pixels), F32),
            pltpu.VMEM((entries, LANES), F32),
            pltpu.VMEM((entries, LANES), F32),
            pltpu.VMEM(block, F32),
            pltpu.VMEM((3, pixels), F32),
            pltpu.VMEM((depths, 3, pixels), F32),
            pltpu.VMEM((tiles,) + block, F32),
            pltpu.VMEM((lines, LANES), F32),
            pltpu.VMEM((lines // 2, LANES), F32),
            pltpu.VMEM((lines // 2, LANES), F32),
            pltpu.VMEM((depths, lines // 2, LANES), F32),
            pltpu.VMEM((lines, LANES), F32),
            dma((tiles,)),
            dma((tiles,)),
            dma((depths,)),
            dma((depths,)),
            dma((2,)),
            dma((2,)),
            dma((depths,)),
            dma((depths,)),
            dma((2,)),
            dma((2,)),
        ],
        name="step",
        compiler_params=pltpu.CompilerParams(
            collective_id=1, has_side_effects=True, vmem_limit_bytes=limit
        ),
    )(*args)
    picture, new_params, new_first, new_second = pl.pallas_call(
        finish_kernel,
        out_shape=[jax.ShapeDtypeStruct(shape, F32) for shape in results],
        in_specs=[pl.BlockSpec(memory_space=pltpu.VMEM)] * len(results),
        out_specs=[pl.BlockSpec(memory_space=pl.ANY)] * len(results),
        scratch_shapes=[dma((len(results),))],
        name="finish",
    )(*[pltpu.with_memory_space_constraint(x, pltpu.VMEM) for x in done])
    return (picture.transpose(1, 0, 2), new_params, new_first, new_second)


def solution(mesh):
    placed = (
        P(None, "tile"),
        P(None, "tile"),
        P(None, "tile"),
        P(None, "tile"),
        P(None, "tile"),
        P(None, "tile"),
        P(),
        P(),
        P("tile", None, None),
        P("tile"),
        P("tile"),
        P("depth", "tile", None, None),
        P("depth", "tile", None),
    )
    return jax.shard_map(
        body,
        mesh=mesh,
        in_specs=placed,
        out_specs=(P("tile", None, None), P(None, "tile"), P(None, "tile"), P(None, "tile")),
        check_vma=False,
    )
```

time: 47.2 us -> 38 us (0.81)
  Pallas kernels: 43.8 us -> 37.2 us
  other arithmetic: 1.81 us -> 0 us
  local copies, waits for them, and re-layouts: 0.65 us -> 0 us
    pallas_call x3 -> x2, Pallas kernels: 43.8 us -> 37.2 us  [the longest x1 36.4 us: body(): pl.pallas_call(functools.partial(step_kernel, tiles, depths), out_shape=[...]
    sub x1 -> x0, other arithmetic: 1.81 us -> none  [adam_update(): return (param - 0.05 * corrected, new_first, new_second)]
    unnamed x13 -> x0, local copies, waits for them, and re-layouts: 0.65 us -> none
where the time goes in v1:
time: 38 us; the launch traced here: 37.9 us
  Pallas kernels  37.2 us (98%)
  between operations  0.64 us (2%)
    pallas_call x1, Pallas kernels, body(): pl.pallas_call(functools.partial(step_kernel, tiles, depths), out_shape=[...  36.4 us
    pallas_call x1, Pallas kernels, body(): pl.pallas_call(finish_kernel, out_shape=[jax.ShapeDtypeStruct(shape, F32)...  0.8 us

profile of v1, /device:TPU:0, one launch (start us, length us, event | category | flops | bytes accessed | tf_op | source)
XLA Modules:
  0.0 37.9 jit_solution(5758719213701828495)
XLA Ops:
  0.6 36.4 %step.1 = (f32[3,4,1024]{2,1,0:T(4,128)S(1)}, f32[10,2048]{1,0:T(8,128)S(1)}, f32[10,2048]{1,0:T(8,128)S(1)}, f32[10,2048]{1,0:T(8,128)S(1)}) custom-call(s32[4,1,128]{2,1,0:T(1,128)} %bitcast.5, s32[4,128]{1,0:T(4,128)} %bitcast.6, f32[3,2048]{1,0:T(4,128)} %place_in.1, f32[3,2048]{1,0:T(4,128)} %scale_in.1, f32[1,2048]{1,0:T(1,128)} %logit_in.1, ...), custom_call_target="tpu_custom_call" | custom-call | tf_op jit(solution)/shard_map/step/pallas_call | solution.py:471
  37.1 0.8 %finish.1 = (f32[3,4,1024]{2,1,0:T(4,128)}, f32[10,2048]{1,0:T(8,128)}, f32[10,2048]{1,0:T(8,128)}, f32[10,2048]{1,0:T(8,128)}) custom-call(f32[3,4,1024]{2,1,0:T(4,128)S(1)} %get-tuple-element.12.refs_0_, f32[10,2048]{1,0:T(8,128)S(1)} %get-tuple-element.13.refs_1_, f32[10,2048]{1,0:T(8,128)S(1)} %get-tuple-element.14.refs_2_, ...), custom_call_target="tpu_custom_call" | custom-call | tf_op jit(solution)/shard_map/finish/pallas_call | solution.py:520

commit v2 on v1

--- a/solution.py
+++ b/solution.py
@@ -12,6 +12,9 @@
 MESH = pl.DeviceIdType.MESH
 F32 = jnp.float32
 BF16 = jnp.bfloat16
+LOG2E = 1.4426950408889634
+PRODUCTS = ((0, 0), (0, 1), (1, 0), (0, 2), (1, 1), (2, 0))
+PULL_ROW, PULL_ROWS = 32, 32
 
 
 def greet(peers):
@@ -57,7 +60,8 @@
     target_ref, view_ref, length_ref, cam_ref, back_ref, loads,
     named_ref, lists_ref, param_ref, high_ref, low_ref, answers, got,
     ask_send, ask_recv, send, receive,
-    alphas, weights, misses, carries, columns, sums, grad_ref, image_ref, images_ref,
+    alphas, weights, pulls, misses, carries, columns, ordered, entry_ref, basis_ref, miss_ref,
+    sums, grad_ref, image_ref, images_ref,
     inbox, partial, half_in, half_sum, pieces, whole_out,
     grad_send, grad_recv, image_send, image_recv, pair_send, pair_recv, cut_send, cut_recv,
     all_send, all_recv,
@@ -112,6 +116,17 @@
     ]
     for copy in copies:
         copy.start()
+    miss_ref[...] = jnp.zeros(miss_ref.shape, BF16)
+    spot = lax.broadcasted_iota(jnp.int32, (1, pixels), 1)
+    spot_x = (spot & (TILE_SIDE - 1)).astype(F32) + (0.5 - 0.5 * TILE_SIDE)
+    spot_y = (spot >> 5).astype(F32) + (0.5 - 0.5 * (pixels // TILE_SIDE))
+    parts = [[jnp.ones((1, pixels), F32)], [spot_x], [spot_y]]
+    for square in (spot_x * spot_x, spot_x * spot_y, spot_y * spot_y):
+        coarse = square.astype(BF16).astype(F32)
+        parts.append([coarse, square - coarse])
+    rows = [part for piece in parts for _ in range(3) for part in piece]
+    rows.append(jnp.zeros((LANES - len(rows), pixels), F32))
+    basis_ref[...] = jnp.concatenate(rows, axis=0).astype(BF16)
     for copy in copies[:2]:
         copy.wait()
     for q in range(slabs):
@@ -172,16 +187,23 @@
             answers.at[step], got.at[step], send.at[step], receive.at[step], across(step)
         )
 
-    def serve(step):
-        for b in range(depths):
-            asked(step, b).wait_recv()
-        put(answers, step, answer(tile_at(step)))
-        back(step).start()
-
-    each_tile(serve)
+    def serve(*group):
+        for step in group:
+            for b in range(depths):
+                asked(step, b).wait_recv()
+        for step in group:
+            put(answers, step, answer(tile_at(step)))
+        for step in group:
+            back(step).start()
+
     for b in range(1, depths):
         asked(0, b).wait_recv()
     put(got, 0, answer(me_t))
+    if small:
+        for step in range(1, tiles, 2):
+            serve(*range(step, min(step + 2, tiles)))
+    else:
+        each_tile(serve)
     for a, b in steps:
         asked(a, b).wait_send()
     for copy in copies[6:]:
@@ -206,9 +228,8 @@
     first = [cam_ref[view, 0, j] for j in range(4)]
     second = [cam_ref[view, 1, j] for j in range(4)]
     variance = [jnp.exp(2.0 * values[3 + j]) for j in range(3)]
-    half = 0.5 * TILE_SIDE
-    center_x = first[0] * values[0] + first[1] * values[1] + first[2] * values[2] + first[3] + half
-    center_y = second[0] * values[0] + second[1] * values[1] + second[2] * values[2] + second[3] + half
+    center_x = first[0] * values[0] + first[1] * values[1] + first[2] * values[2] + first[3]
+    center_y = second[0] * values[0] + second[1] * values[1] + second[2] * values[2] + second[3]
     cov_xx = sum(first[j] * first[j] * variance[j] for j in range(3)) + 0.3
     cov_xy = sum(first[j] * second[j] * variance[j] for j in range(3))
     cov_yy = sum(second[j] * second[j] * variance[j] for j in range(3)) + 0.3
@@ -216,19 +237,46 @@
     conic_a = cov_yy / determinant
     conic_b = -cov_xy / determinant
     conic_c = cov_xx / determinant
-    opacity = 1.0 / (1.0 + jnp.exp(-values[6]))
+    fade = 1.0 + jnp.exp(-values[6])
+    opacity = 1.0 / fade
     place = lax.broadcasted_iota(jnp.int32, (1, entries), 1)
-    shown = jnp.where(place < length, opacity, 0.0)
-    rows = [center_x, center_y, -0.5 * conic_a, -conic_b, -0.5 * conic_c, shown] + values[7:10]
-    table = jnp.concatenate(rows + [jnp.zeros((LANES - len(rows), entries), F32)], axis=0)
-    columns[...] = table.T
+    slope_x = conic_a * center_x + conic_b * center_y
+    slope_y = conic_b * center_x + conic_c * center_y
+    level = -0.5 * (slope_x * center_x + slope_y * center_y) - jnp.log(fade)
+    terms = [
+        jnp.where(place < length, LOG2E * level, -1e30),
+        LOG2E * slope_x, LOG2E * slope_y,
+        (-0.5 * LOG2E) * conic_a, -LOG2E * conic_b, (-0.5 * LOG2E) * conic_c,
+    ]
+    rows = []
+    for term, copies_of in zip(terms, (1, 1, 1, 2, 2, 2)):
+        for piece in split3(term):
+            rows += [piece.astype(F32)] * copies_of
+    rows += [jnp.zeros((PULL_ROW - len(rows), entries), F32)]
+    for k in range(3):
+        pieces_of = split3(values[7 + k])
+        rows += [pieces_of[i].astype(F32) for i, _ in PRODUCTS]
+    rows += values[7:10]
+    rows += [jnp.zeros((LANES - PULL_ROW - 3 * len(PRODUCTS) - 3, entries), F32)]
+    columns[...] = jnp.concatenate(rows, axis=0).T
+    for g in range(groups):
+        block = columns[pl.ds(g, 8, stride=groups), :]
+        ordered[g * 8 : (g + 1) * 8, :] = block
+    entry_ref[...] = ordered[...].astype(BF16)
+    width = 2 * LANES
+    for n in range(pixels // width):
+        part = slice(n * width, (n + 1) * width)
+        alphas[:, part] = jnp.exp2(
+            jnp.dot(entry_ref[...], basis_ref[:, part], preferred_element_type=F32)
+        )
 
     lane = lax.broadcasted_iota(jnp.int32, (8, LANES), 1)
     sub = lax.broadcasted_iota(jnp.int32, (8, LANES), 0)
-    pixel_x = (lane & (TILE_SIDE - 1)).astype(F32) + 0.5
-    pixel_y = (lane >> 5).astype(F32) + 0.5
     rows_chunk = LANES // TILE_SIDE
+    pixel_x = (lane & (TILE_SIDE - 1)).astype(F32) + (0.5 - 0.5 * TILE_SIDE)
+    pixel_y = (lane >> 5).astype(F32) - 0.5 * (rows_chunk - 1)
     ones = jnp.ones((8, LANES), F32)
+    tint = PULL_ROW + 3 * len(PRODUCTS)
 
     def spread(cols, j):
         return jnp.broadcast_to(cols[:, j : j + 1], (8, LANES))
@@ -236,20 +284,13 @@
     def forward(g, carry):
         trans, color = carry
         at = pl.ds(pl.multiple_of(g * 8, 8), 8)
-        cols = columns[pl.ds(g, 8, stride=groups), :]
-        cx, cy, qa, qb, qc, op, red, green, blue = [spread(cols, j) for j in range(9)]
-        ex = pixel_x - cx
-        ey0 = pixel_y - cy
-        qaxx = qa * ex * ex
-        qbx = qb * ex
+        cols = ordered[at, :]
+        red, green, blue = [spread(cols, tint + j) for j in range(3)]
         new_trans, new_color = [], []
         for c in range(chunks):
-            ey = ey0 + float(c * rows_chunk)
-            alpha = op * jnp.exp(qaxx + (qbx + qc * ey) * ey)
             t = trans[c]
             part = slice(c * LANES, (c + 1) * LANES)
-            alphas[at, part] = alpha
-            weight = alpha * t
+            weight = alphas[at, part] * t
             weights[at, part] = weight
             new_trans.append(t - weight)
             new_color.append(color[3 * c] + weight * red)
@@ -271,23 +312,26 @@
             run = run * jnp.where(sub >= s, pltpu.roll(run, s, 0), 1.0)
         carries[:, part] = run
         left = (run * trans[c])[7:8, :]
-        total = 0.0
         pulled = zeros
+        last = zeros[0:1]
         for k in range(3):
-            lit = run * color[3 * c + k]
-            shade = jnp.sum(lit, axis=0, keepdims=True) + left * back_ref[k]
+            shade = jnp.sum(run * color[3 * c + k], axis=0, keepdims=True) + left * back_ref[k]
             image_ref[k : k + 1, part] = shade
             miss = shade - jnp.sum(
                 jnp.where(chosen, target_ref[k, :, part], 0.0), axis=0, keepdims=True
             )
             misses[k, :, part] = jnp.broadcast_to(miss, (8, LANES))
-            total = total + miss * shade
-            pulled = pulled + miss * lit
-        ahead = jnp.where(sub >= 1, pltpu.roll(pulled, 1, 0), 0.0)
+            pulled = pulled + miss * color[3 * c + k]
+            last = last + miss * back_ref[k]
+        kept = trans[c]
         for s in (1, 2, 4):
-            ahead = ahead + jnp.where(sub >= s, pltpu.roll(ahead, s, 0), 0.0)
-        behinds.append(total - ahead)
-
+            inner = sub < 8 - s
+            pulled = pulled + kept * jnp.where(inner, pltpu.roll(pulled, 8 - s, 0), 0.0)
+            kept = kept * jnp.where(inner, pltpu.roll(kept, 8 - s, 0), 1.0)
+        begins = pulled + kept * last
+        behinds.append(
+            jnp.where(sub < 7, pltpu.roll(begins, 7, 0), jnp.broadcast_to(last, (8, LANES)))
+        )
     images_ref[me_d] = image_ref[...]
     image_copies = [
         remote(image_ref, images_ref.at[me_d], image_send.at[s], image_recv.at[s], along(s))
@@ -295,45 +339,58 @@
     ]
     for copy in image_copies:
         copy.start()
-
-    def backward(g, behind):
+    rows = []
+    for k in range(3):
+        pieces_of = split3(misses[k, 0:1, :])
+        rows += [pieces_of[j].astype(F32) for _, j in PRODUCTS]
+    rows += [jnp.zeros((PULL_ROWS - len(rows), pixels), F32)]
+    miss_ref[PULL_ROW : PULL_ROW + PULL_ROWS, :] = jnp.concatenate(rows, axis=0).astype(BF16)
+    for n in range(pixels // width):
+        part = slice(n * width, (n + 1) * width)
+        pulls[:, part] = jnp.dot(entry_ref[...], miss_ref[:, part], preferred_element_type=F32)
+
+    def backward(i, behind):
+        g = groups - 1 - i
         at = pl.ds(pl.multiple_of(g * 8, 8), 8)
-        spaced = pl.ds(g, 8, stride=groups)
-        cols = columns[spaced, :]
-        cx, cy, red, green, blue = [spread(cols, j) for j in (0, 1, 6, 7, 8)]
-        ex = pixel_x - cx
-        ey0 = pixel_y - cy
-        new_behind = []
-        acc = [zeros] * 6
+        new_behind, grad = [], []
+        shades = [zeros] * 3
         for c in range(chunks):
             part = slice(c * LANES, (c + 1) * LANES)
-            alpha = alphas[at, part]
             weight = weights[at, part] * carries[:, part]
-            m0, m1, m2 = misses[0, :, part], misses[1, :, part], misses[2, :, part]
-            pull = m0 * red + m1 * green + m2 * blue
-            rest = behind[c] - weight * pull
-            new_behind.append(rest)
-            grad = weight * pull - rest * (alpha / (1.0 - alpha))
-            ey = ey0 + float(c * rows_chunk)
-            gy = grad * ey
-            acc[0] = acc[0] + grad
-            acc[1] = acc[1] + gy
-            acc[2] = acc[2] + gy * ey
-            acc[3] = acc[3] + weight * m0
-            acc[4] = acc[4] + weight * m1
-            acc[5] = acc[5] + weight * m2
-        gx = acc[0] * ex
-        fields = [acc[0], gx, acc[1], gx * ex, acc[1] * ex, acc[2], acc[3], acc[4], acc[5]]
+            gap = pulls[at, part] - behind[c]
+            new_behind.append(behind[c] + alphas[at, part] * gap)
+            grad.append(weight * gap)
+            shades = [shades[k] + weight * misses[k, :, part] for k in range(3)]
+        sum_0, sum_1, sum_2 = zeros, zeros, zeros
+        for c in range(chunks // 2):
+            low, high = grad[c], grad[chunks - 1 - c]
+            off = float(rows_chunk) * (0.5 * (chunks - 1) - c)
+            even, odd = low + high, high - low
+            sum_0 = sum_0 + even
+            sum_1 = sum_1 + off * odd
+            sum_2 = sum_2 + (off * off) * even
+        down = sum_1 + pixel_y * sum_0
+        down_2 = sum_2 + pixel_y * (sum_1 + down)
+        right = sum_0 * pixel_x
+        fields = [sum_0, right, down, right * pixel_x, down * pixel_x, down_2] + shades
         packed = zeros
         for j, field in enumerate(fields):
             packed = jnp.where(lane == j, jnp.sum(field, axis=1, keepdims=True), packed)
-        sums[spaced, :] = packed
+        sums[pl.ds(g, 8, stride=groups), :] = packed
         return new_behind
 
     lax.fori_loop(0, groups, backward, behinds, unroll=4)
 
     flat = sums[...].T
     s0, sx, sy, sxx, sxy, syy, d_red, d_green, d_blue = [flat[j : j + 1, :] for j in range(9)]
+    sxx = sxx - center_x * sx
+    sxy = sxy - center_x * sy
+    syy = syy - center_y * sy
+    sx = sx - center_x * s0
+    sy = sy - center_y * s0
+    sxx = sxx - center_x * sx
+    sxy = sxy - center_y * sx
+    syy = syy - center_y * sy
     d_x = conic_a * sx + conic_b * sy
     d_y = conic_b * sx + conic_c * sy
     d_a, d_b, d_c = -0.5 * sxx, -sxy, -0.5 * syy
@@ -488,9 +545,14 @@
             dma((tiles,)),
             pltpu.VMEM((entries, pixels), F32),
             pltpu.VMEM((entries, pixels), F32),
+            pltpu.VMEM((entries, pixels), F32),
             pltpu.VMEM((3, 8, pixels), F32),
             pltpu.VMEM((8, pixels), F32),
             pltpu.VMEM((entries, LANES), F32),
+            pltpu.VMEM((entries, LANES), F32),
+            pltpu.VMEM((entries, LANES), BF16),
+            pltpu.VMEM((LANES, pixels), BF16),
+            pltpu.VMEM((LANES, pixels), BF16),
             pltpu.VMEM((entries, LANES), F32),
             pltpu.VMEM(block, F32),
             pltpu.VMEM((3, pixels), F32),

time: 38 us -> 36.4 us (0.958)
  Pallas kernels: 37.2 us -> 35.6 us
    pallas_call x1, Pallas kernels: 36.4 us -> 34.8 us  [body(): pl.pallas_call(functools.partial(step_kernel, tiles, depths), out_shape=[...]
where the time goes in v2:
time: 36.4 us; the launch traced here: 36.3 us
  Pallas kernels  35.6 us (98%)
  between operations  0.64 us (2%)
    pallas_call x1, Pallas kernels, body(): pl.pallas_call(functools.partial(step_kernel, tiles, depths), out_shape=[...  34.8 us
    pallas_call x1, Pallas kernels, body(): pl.pallas_call(finish_kernel, out_shape=[jax.ShapeDtypeStruct(shape, F32)...  0.8 us

profile of v2, /device:TPU:0, one launch (start us, length us, event | category | flops | bytes accessed | tf_op | source)
XLA Modules:
  0.0 36.3 jit_solution(3243317298722649936)
XLA Ops:
  0.6 34.8 %step.1 = (f32[3,4,1024]{2,1,0:T(4,128)S(1)}, f32[10,2048]{1,0:T(8,128)S(1)}, f32[10,2048]{1,0:T(8,128)S(1)}, f32[10,2048]{1,0:T(8,128)S(1)}) custom-call(s32[4,1,128]{2,1,0:T(1,128)} %bitcast.5, s32[4,128]{1,0:T(4,128)} %bitcast.6, f32[3,2048]{1,0:T(4,128)} %place_in.1, f32[3,2048]{1,0:T(4,128)} %scale_in.1, f32[1,2048]{1,0:T(1,128)} %logit_in.1, ...), custom_call_target="tpu_custom_call" | custom-call | tf_op jit(solution)/shard_map/step/pallas_call | solution.py:528
  35.5 0.8 %finish.1 = (f32[3,4,1024]{2,1,0:T(4,128)}, f32[10,2048]{1,0:T(8,128)}, f32[10,2048]{1,0:T(8,128)}, f32[10,2048]{1,0:T(8,128)}) custom-call(f32[3,4,1024]{2,1,0:T(4,128)S(1)} %get-tuple-element.12.refs_0_, f32[10,2048]{1,0:T(8,128)S(1)} %get-tuple-element.13.refs_1_, f32[10,2048]{1,0:T(8,128)S(1)} %get-tuple-element.14.refs_2_, ...), custom_call_target="tpu_custom_call" | custom-call | tf_op jit(solution)/shard_map/finish/pallas_call | solution.py:582

commit v3 on v2

--- a/solution.py
+++ b/solution.py
@@ -15,6 +15,7 @@
 LOG2E = 1.4426950408889634
 PRODUCTS = ((0, 0), (0, 1), (1, 0), (0, 2), (1, 1), (2, 0))
 PULL_ROW, PULL_ROWS = 32, 32
+UNROLL = 16
 
 
 def greet(peers):
@@ -58,13 +59,13 @@
     picture_ref, new_param_ref, new_first_ref, new_second_ref,
     owner_ref, row_ref, place_ref, scale_ref, logit_ref, color_ref, first_ref, second_ref,
     target_ref, view_ref, length_ref, cam_ref, back_ref, loads,
-    named_ref, lists_ref, param_ref, high_ref, low_ref, answers, got,
+    named_ref, lists_ref, twin_ref, hot_ref, high_names, first_lines, second_lines, twin_sem,
+    param_ref, high_ref, low_ref, answers, got,
     ask_send, ask_recv, send, receive,
     alphas, weights, pulls, misses, carries, columns, ordered, entry_ref, basis_ref, miss_ref,
     sums, grad_ref, image_ref, images_ref,
-    inbox, partial, half_in, half_sum, pieces, whole_out,
-    grad_send, grad_recv, image_send, image_recv, pair_send, pair_recv, cut_send, cut_recv,
-    all_send, all_recv,
+    inbox, partial, pieces, whole_out,
+    grad_send, grad_recv, image_send, image_recv, cut_send, cut_recv, pair_sem,
 ):
     lines = param_ref.shape[0]
     highs = lines // 10
@@ -129,8 +130,14 @@
     basis_ref[...] = jnp.concatenate(rows, axis=0).astype(BF16)
     for copy in copies[:2]:
         copy.wait()
+    names = jnp.concatenate([owner_ref[q] for q in range(slabs)], axis=0) * splats + row_ref[...]
+    quad = lax.broadcasted_iota(jnp.int32, names.shape, 1) >> ((slab // 4).bit_length() - 1)
+    names = jnp.where(
+        quad == 1, pltpu.roll(names, 3 * slab // 4, 1),
+        jnp.where(quad == 2, pltpu.roll(names, slab // 4, 1), names),
+    )
     for q in range(slabs):
-        named_ref[q] = owner_ref[q] * splats + row_ref[q : q + 1, :]
+        named_ref[q] = names[q : q + 1, :]
     pl.semaphore_wait(barrier, len(steps))
 
     def asked(a, b):
@@ -156,14 +163,32 @@
     low_ref[...] = low
     low_iota = lax.broadcasted_iota(jnp.int32, (LANES, entries), 0)
     high_iota = lax.broadcasted_iota(jnp.int32, (highs, entries), 0) + me_t * highs
-
-    def entry_names(slot):
-        names = jnp.concatenate([lists_ref[slot, d] for d in range(slabs)], axis=1)
+    span = entries // 2
+    early = lax.broadcasted_iota(jnp.int32, (1, slab), 1) < slab // 2
+
+    def widen(ref, slot):
+        slab_names = [ref[slot, d] for d in range(slabs)]
+        turned = [pltpu.roll(x, slab // 2, 1) for x in slab_names]
+        return [
+            jnp.where(early, slab_names[d], turned[d + 1]) for d in range(0, slabs, 2)
+        ] + [
+            jnp.where(early, turned[d], slab_names[d + 1]) for d in range(0, slabs, 2)
+        ]
+
+    def marks(names):
         onehot = jnp.where(low_iota == (names & (LANES - 1)), 1.0, 0.0).astype(BF16)
         return onehot, high_iota == (names >> 7)
 
-    def answer(slot):
-        onehot, mask = entry_names(slot)
+    def note(source, step, names):
+        onehot, mask = marks(names)
+        for part in range(2):
+            cut = slice(part * span, (part + 1) * span)
+            hot_ref[source, step, part] = onehot[:, cut]
+            high_names[source, step, part] = names[:, cut] >> 7
+        return onehot, mask
+
+    def answer(step):
+        onehot, mask = note(0, step, jnp.concatenate(widen(lists_ref, tile_at(step)), axis=1))
         twice = jnp.concatenate([onehot, onehot], axis=0)
         found = jnp.dot(high_ref[...], twice, preferred_element_type=F32) + jnp.dot(
             low_ref[...], onehot, preferred_element_type=F32
@@ -180,11 +205,15 @@
 
     def put(ref, step, rows):
         for j in range(slabs):
-            ref[step, j * 10 : (j + 1) * 10, :] = rows[:, j * slab : (j + 1) * slab]
-
-    def back(step):
+            k = j % (slabs // 2)
+            ref[step, j // (slabs // 2), k * 10 : (k + 1) * 10, :] = rows[
+                :, j * slab : (j + 1) * slab
+            ]
+
+    def back(step, part):
         return remote(
-            answers.at[step], got.at[step], send.at[step], receive.at[step], across(step)
+            answers.at[step, part], got.at[step, part], send.at[step, part],
+            receive.at[step, part], across(step),
         )
 
     def serve(*group):
@@ -192,83 +221,109 @@
             for b in range(depths):
                 asked(step, b).wait_recv()
         for step in group:
-            put(answers, step, answer(tile_at(step)))
+            put(answers, step, answer(step))
         for step in group:
-            back(step).start()
+            back(step, 0).start()
 
     for b in range(1, depths):
         asked(0, b).wait_recv()
-    put(got, 0, answer(me_t))
+    put(got, 0, answer(0))
     if small:
         for step in range(1, tiles, 2):
             serve(*range(step, min(step + 2, tiles)))
     else:
         each_tile(serve)
+    each_tile(lambda step: back(step, 1).start())
+    twin = remote(lists_ref, twin_ref, twin_sem.at[0], twin_sem.at[1], along(1))
+    twin.start()
     for a, b in steps:
         asked(a, b).wait_send()
     for copy in copies[6:]:
         copy.wait()
-
-    def take(step):
-        back(step).wait()
-        got[0] += got[step]
-
-    each_tile(take)
-    found = got[0]
+    for h in range(highs):
+        spaced = pl.ds(h, 10, stride=highs)
+        first_lines[spaced, :] = first_ref[:, h * LANES : (h + 1) * LANES]
+        second_lines[spaced, :] = second_ref[:, h * LANES : (h + 1) * LANES]
+    twin.wait()
+
+    def note_twin(step):
+        note(1, step, jnp.concatenate(widen(twin_ref, tile_at(step)), axis=1))
+
+    note_twin(0)
+    each_tile(note_twin)
 
     chunks = pixels // LANES
     groups = entries // 8
     length = length_ref[me_d]
     view = view_ref[me_d]
-    values = [
-        jnp.concatenate([found[j * 10 + p : j * 10 + p + 1, :] for j in range(slabs)], axis=1)
-        for p in range(10)
-    ]
 
     first = [cam_ref[view, 0, j] for j in range(4)]
     second = [cam_ref[view, 1, j] for j in range(4)]
-    variance = [jnp.exp(2.0 * values[3 + j]) for j in range(3)]
-    center_x = first[0] * values[0] + first[1] * values[1] + first[2] * values[2] + first[3]
-    center_y = second[0] * values[0] + second[1] * values[1] + second[2] * values[2] + second[3]
-    cov_xx = sum(first[j] * first[j] * variance[j] for j in range(3)) + 0.3
-    cov_xy = sum(first[j] * second[j] * variance[j] for j in range(3))
-    cov_yy = sum(second[j] * second[j] * variance[j] for j in range(3)) + 0.3
-    determinant = cov_xx * cov_yy - cov_xy * cov_xy
-    conic_a = cov_yy / determinant
-    conic_b = -cov_xy / determinant
-    conic_c = cov_xx / determinant
-    fade = 1.0 + jnp.exp(-values[6])
-    opacity = 1.0 / fade
-    place = lax.broadcasted_iota(jnp.int32, (1, entries), 1)
-    slope_x = conic_a * center_x + conic_b * center_y
-    slope_y = conic_b * center_x + conic_c * center_y
-    level = -0.5 * (slope_x * center_x + slope_y * center_y) - jnp.log(fade)
-    terms = [
-        jnp.where(place < length, LOG2E * level, -1e30),
-        LOG2E * slope_x, LOG2E * slope_y,
-        (-0.5 * LOG2E) * conic_a, -LOG2E * conic_b, (-0.5 * LOG2E) * conic_c,
-    ]
-    rows = []
-    for term, copies_of in zip(terms, (1, 1, 1, 2, 2, 2)):
-        for piece in split3(term):
-            rows += [piece.astype(F32)] * copies_of
-    rows += [jnp.zeros((PULL_ROW - len(rows), entries), F32)]
-    for k in range(3):
-        pieces_of = split3(values[7 + k])
-        rows += [pieces_of[i].astype(F32) for i, _ in PRODUCTS]
-    rows += values[7:10]
-    rows += [jnp.zeros((LANES - PULL_ROW - 3 * len(PRODUCTS) - 3, entries), F32)]
-    columns[...] = jnp.concatenate(rows, axis=0).T
-    for g in range(groups):
-        block = columns[pl.ds(g, 8, stride=groups), :]
-        ordered[g * 8 : (g + 1) * 8, :] = block
-    entry_ref[...] = ordered[...].astype(BF16)
     width = 2 * LANES
-    for n in range(pixels // width):
-        part = slice(n * width, (n + 1) * width)
-        alphas[:, part] = jnp.exp2(
-            jnp.dot(entry_ref[...], basis_ref[:, part], preferred_element_type=F32)
-        )
+
+    def project(part):
+        def take(step):
+            back(step, part).wait()
+            got[0, part] += got[step, part]
+
+        each_tile(take)
+        found = got[0, part]
+        values = [
+            jnp.concatenate(
+                [found[j * 10 + p : j * 10 + p + 1, :] for j in range(slabs // 2)], axis=1
+            )
+            for p in range(10)
+        ]
+        variance = [jnp.exp(2.0 * values[3 + j]) for j in range(3)]
+        center_x = first[0] * values[0] + first[1] * values[1] + first[2] * values[2] + first[3]
+        center_y = second[0] * values[0] + second[1] * values[1] + second[2] * values[2] + second[3]
+        cov_xx = sum(first[j] * first[j] * variance[j] for j in range(3)) + 0.3
+        cov_xy = sum(first[j] * second[j] * variance[j] for j in range(3))
+        cov_yy = sum(second[j] * second[j] * variance[j] for j in range(3)) + 0.3
+        determinant = cov_xx * cov_yy - cov_xy * cov_xy
+        conic_a = cov_yy / determinant
+        conic_b = -cov_xy / determinant
+        conic_c = cov_xx / determinant
+        fade = 1.0 + jnp.exp(-values[6])
+        opacity = 1.0 / fade
+        spot = lax.broadcasted_iota(jnp.int32, (1, span), 1)
+        stretch = groups // 2
+        place = (
+            (spot >> (stretch.bit_length() - 1)) * groups + part * stretch + (spot & (stretch - 1))
+        )
+        slope_x = conic_a * center_x + conic_b * center_y
+        slope_y = conic_b * center_x + conic_c * center_y
+        level = -0.5 * (slope_x * center_x + slope_y * center_y) - jnp.log(fade)
+        terms = [
+            jnp.where(place < length, LOG2E * level, -1e30),
+            LOG2E * slope_x, LOG2E * slope_y,
+            (-0.5 * LOG2E) * conic_a, -LOG2E * conic_b, (-0.5 * LOG2E) * conic_c,
+        ]
+        rows = []
+        for term, copies_of in zip(terms, (1, 1, 1, 2, 2, 2)):
+            for piece in split3(term):
+                rows += [piece.astype(F32)] * copies_of
+        rows += [jnp.zeros((PULL_ROW - len(rows), span), F32)]
+        for k in range(3):
+            pieces_of = split3(values[7 + k])
+            rows += [pieces_of[i].astype(F32) for i, _ in PRODUCTS]
+        rows += values[7:10]
+        rows += [jnp.zeros((LANES - PULL_ROW - 3 * len(PRODUCTS) - 3, span), F32)]
+        base = part * span
+        columns[base : base + span, :] = jnp.concatenate(rows, axis=0).T
+        for g in range(stretch):
+            ordered[base + g * 8 : base + (g + 1) * 8, :] = columns[
+                pl.ds(base + g, 8, stride=stretch), :
+            ]
+        entry_ref[base : base + span, :] = ordered[base : base + span, :].astype(BF16)
+        for n in range(pixels // width):
+            cut = slice(n * width, (n + 1) * width)
+            alphas[base : base + span, cut] = jnp.exp2(
+                jnp.dot(
+                    entry_ref[base : base + span, :], basis_ref[:, cut], preferred_element_type=F32
+                )
+            )
+        return variance, center_x, center_y, conic_a, conic_b, conic_c, opacity
 
     lane = lax.broadcasted_iota(jnp.int32, (8, LANES), 1)
     sub = lax.broadcasted_iota(jnp.int32, (8, LANES), 0)
@@ -299,9 +354,14 @@
         return new_trans, new_color
 
     zeros = jnp.zeros((8, LANES), F32)
-    trans, color = lax.fori_loop(
-        0, groups, forward, ([ones] * chunks, [zeros] * (3 * chunks)), unroll=4
-    )
+    carried = ([ones] * chunks, [zeros] * (3 * chunks))
+    screens = []
+    for part in range(2):
+        screens.append(project(part))
+        carried = lax.fori_loop(
+            part * (groups // 2), (part + 1) * (groups // 2), forward, carried, unroll=UNROLL
+        )
+    trans, color = carried
 
     chosen = lax.broadcasted_iota(jnp.int32, (slabs, LANES), 0) == me_d
     behinds = []
@@ -349,8 +409,7 @@
         part = slice(n * width, (n + 1) * width)
         pulls[:, part] = jnp.dot(entry_ref[...], miss_ref[:, part], preferred_element_type=F32)
 
-    def backward(i, behind):
-        g = groups - 1 - i
+    def backward(g, behind, piece):
         at = pl.ds(pl.multiple_of(g * 8, 8), 8)
         new_behind, grad = [], []
         shades = [zeros] * 3
@@ -376,96 +435,121 @@
         packed = zeros
         for j, field in enumerate(fields):
             packed = jnp.where(lane == j, jnp.sum(field, axis=1, keepdims=True), packed)
-        sums[pl.ds(g, 8, stride=groups), :] = packed
+        stretch = groups // 2
+        sums[pl.ds(piece * (span - stretch) + g, 8, stride=stretch), :] = packed
         return new_behind
 
-    lax.fori_loop(0, groups, backward, behinds, unroll=4)
-
-    flat = sums[...].T
-    s0, sx, sy, sxx, sxy, syy, d_red, d_green, d_blue = [flat[j : j + 1, :] for j in range(9)]
-    sxx = sxx - center_x * sx
-    sxy = sxy - center_x * sy
-    syy = syy - center_y * sy
-    sx = sx - center_x * s0
-    sy = sy - center_y * s0
-    sxx = sxx - center_x * sx
-    sxy = sxy - center_y * sx
-    syy = syy - center_y * sy
-    d_x = conic_a * sx + conic_b * sy
-    d_y = conic_b * sx + conic_c * sy
-    d_a, d_b, d_c = -0.5 * sxx, -sxy, -0.5 * syy
-    d_xx = -(conic_a * conic_a * d_a + conic_a * conic_b * d_b + conic_b * conic_b * d_c)
-    d_yy = -(conic_b * conic_b * d_a + conic_b * conic_c * d_b + conic_c * conic_c * d_c)
-    d_xy = -(
-        2.0 * conic_a * conic_b * d_a
-        + (conic_a * conic_c + conic_b * conic_b) * d_b
-        + 2.0 * conic_b * conic_c * d_c
-    )
-    out = [first[j] * d_x + second[j] * d_y for j in range(3)]
-    for j in range(3):
-        d_var = first[j] * first[j] * d_xx + first[j] * second[j] * d_xy + second[j] * second[j] * d_yy
-        out.append(2.0 * variance[j] * d_var)
-    out += [s0 * (1.0 - opacity), d_red, d_green, d_blue]
-    out = jnp.concatenate(out, axis=0)
-    for j in range(slabs):
-        grad_ref[j * 10 : (j + 1) * 10, :] = out[:, j * slab : (j + 1) * slab]
-
-    def grads(step):
+    core = lax.rem(me_d, 2)
+
+    def grads(step, other, part):
         return remote(
-            grad_ref, inbox.at[step], grad_send.at[step], grad_recv.at[step], across(step)
-        )
-
-    for step in range(tiles - 1, 0, -1):
-        grads(step).start()
-
-    def placed(block, slot):
-        onehot, mask = entry_names(slot)
-        wide = jnp.concatenate([block[j * 10 : (j + 1) * 10, :] for j in range(slabs)], axis=1)
-        spots = jnp.concatenate(
-            [jnp.where(mask, wide[p : p + 1, :], 0.0) for p in range(10)], axis=0
-        )
-        high = spots.astype(BF16)
-        middle = (spots - high.astype(F32)).astype(BF16)
+            grad_ref.at[part, core if not other else 1 - core], inbox.at[step, other, part],
+            grad_send.at[step, other, part], grad_recv.at[step, other, part],
+            to(step, other),
+        )
+
+    ways = [(step, other) for step in range(tiles - 1, -1, -1) for other in (0, 1) if step or other]
+    for part in (1, 0):
+        top = (part + 1) * (groups // 2)
+        behinds = lax.fori_loop(
+            0, groups // 2, lambda i, behind: backward(top - 1 - i, behind, part), behinds,
+            unroll=UNROLL,
+        )
+        variance, center_x, center_y, conic_a, conic_b, conic_c, opacity = screens[part]
+        flat = sums[part * span : (part + 1) * span, :].T
+        s0, sx, sy, sxx, sxy, syy, d_red, d_green, d_blue = [flat[j : j + 1, :] for j in range(9)]
+        sxx = sxx - center_x * sx
+        sxy = sxy - center_x * sy
+        syy = syy - center_y * sy
+        sx = sx - center_x * s0
+        sy = sy - center_y * s0
+        sxx = sxx - center_x * sx
+        sxy = sxy - center_y * sx
+        syy = syy - center_y * sy
+        d_x = conic_a * sx + conic_b * sy
+        d_y = conic_b * sx + conic_c * sy
+        d_a, d_b, d_c = -0.5 * sxx, -sxy, -0.5 * syy
+        d_xx = -(conic_a * conic_a * d_a + conic_a * conic_b * d_b + conic_b * conic_b * d_c)
+        d_yy = -(conic_b * conic_b * d_a + conic_b * conic_c * d_b + conic_c * conic_c * d_c)
+        d_xy = -(
+            2.0 * conic_a * conic_b * d_a
+            + (conic_a * conic_c + conic_b * conic_b) * d_b
+            + 2.0 * conic_b * conic_c * d_c
+        )
+        out = [first[j] * d_x + second[j] * d_y for j in range(3)]
+        for j in range(3):
+            d_var = first[j] * first[j] * d_xx + first[j] * second[j] * d_xy + second[j] * second[j] * d_yy
+            out.append(2.0 * variance[j] * d_var)
+        out += [s0 * (1.0 - opacity), d_red, d_green, d_blue]
+        out = jnp.concatenate(out, axis=0)
+        for u in range(2):
+            for j in range(slabs // 2):
+                grad_ref[part, u, j * 5 : (j + 1) * 5, :] = out[
+                    u * 5 : (u + 1) * 5, j * slab : (j + 1) * slab
+                ]
+        for step, other in ways:
+            grads(step, other, part).start()
+
+    size = lines // 2
+
+    def placed(blocks, step, part):
         dims = (((1,), (1,)), ((), ()))
-        return lax.dot_general(
-            high, onehot, dims, preferred_element_type=F32
-        ) + lax.dot_general(middle, onehot, dims, preferred_element_type=F32)
-
-    partial[...] = placed(grad_ref[...], me_t)
-
-    def add(step):
-        grads(step).wait()
-        partial[...] += placed(inbox[step], tile_at(step))
-
-    each_tile(add)
-
-    size = lines // 2
+        total = 0.0
+        for source, block in enumerate(blocks):
+            wide = jnp.concatenate(
+                [block[j * 5 : (j + 1) * 5, :] for j in range(slabs // 2)], axis=1
+            )
+            mask = high_iota[:, :span] == high_names[source, step, part]
+            high = wide.astype(BF16).astype(F32)
+            for rows in (high, wide - high):
+                spots = jnp.concatenate(
+                    [jnp.where(mask, rows[p : p + 1, :], 0.0) for p in range(5)], axis=0
+                )
+                total = total + lax.dot_general(
+                    spots.astype(BF16), hot_ref[source, step, part], dims,
+                    preferred_element_type=F32,
+                )
+        return total
+
+    partial[...] = jnp.zeros(partial.shape, F32)
+    for part in (1, 0):
+        grads(0, 1, part).wait()
+        partial[...] += placed([grad_ref[part, core], inbox[0, 1, part]], 0, part)
+
+        def add(step):
+            for other in (0, 1):
+                grads(step, other, part).wait()
+            partial[...] += placed([inbox[step, 0, part], inbox[step, 1, part]], step, part)
+
+        each_tile(add)
 
     def side(index):
         return pl.ds(pl.multiple_of(index * size, 8), size)
 
-    core = lax.rem(me_d, 2)
-    mine, other = side(core), side(1 - core)
-    pair = remote(partial.at[other], half_in, pair_send.at[0], pair_recv.at[0], along(1))
-    pair.start()
-    pair.wait()
-    half_sum[...] = partial[mine, :] + half_in[...]
+    mine = side(core)
     cuts = [
-        remote(half_sum, pieces.at[s], cut_send.at[s], cut_recv.at[s], along(s))
+        remote(partial, pieces.at[s], cut_send.at[s], cut_recv.at[s], along(s))
         for s in range(2, depths, 2)
     ]
     for copy in cuts:
         copy.start()
-    total = half_sum[...]
+    total = partial[...]
     for copy in cuts:
         copy.wait_recv()
     for s in range(2, depths, 2):
         total = total + pieces[s]
     whole_out[mine, :] = total
     share = remote(
-        whole_out.at[mine], whole_out.at[mine], pair_send.at[1], pair_recv.at[1], along(1)
+        whole_out.at[mine], whole_out.at[mine], pair_sem.at[0], pair_sem.at[1], along(1)
     )
     share.start()
+
+    def finish(rows):
+        param_ref[rows, :], first_lines[rows, :], second_lines[rows, :] = adam_update(
+            param_ref[rows, :], first_lines[rows, :], second_lines[rows, :], whole_out[rows, :]
+        )
+
+    finish(mine)
     for copy in cuts:
         copy.wait_send()
     for copy in image_copies:
@@ -474,12 +558,13 @@
         for k in range(3):
             picture_ref[k, d : d + 1, :] = images_ref[d, k : k + 1, :]
     share.wait()
+    finish(side(1 - core))
     for h in range(highs):
         part = slice(h * LANES, (h + 1) * LANES)
         spaced = pl.ds(h, 10, stride=highs)
-        new_param_ref[:, part], new_first_ref[:, part], new_second_ref[:, part] = adam_update(
-            param_ref[spaced, :], first_ref[:, part], second_ref[:, part], whole_out[spaced, :]
-        )
+        new_param_ref[:, part] = param_ref[spaced, :]
+        new_first_ref[:, part] = first_lines[spaced, :]
+        new_second_ref[:, part] = second_lines[spaced, :]
 
 
 def adam_update(param, first, second, gradient):
@@ -511,10 +596,11 @@
     entries = slab * depths
     splats = positions.shape[1]
     lines = 10 * splats // LANES
-    assert tiles_here == depths and slab == LANES and depths % 2 == 0
+    assert tiles_here == depths == 4 and slab == LANES
     assert tiles & (tiles - 1) == 0 and depths & (depths - 1) == 0
     dma = pltpu.SemaphoreType.DMA
-    block = (10 * depths, slab)
+    block = (5 * depths, slab)
+    slip = (5 * depths // 2, slab)
     limit = 60 << 20
     args = [
         list_owner.reshape(tiles_here, 1, slab), list_row[0],
@@ -534,15 +620,21 @@
             dma((len(args),)),
             pltpu.VMEM((depths, 1, slab), jnp.int32),
             pltpu.VMEM((tiles, depths, 1, slab), jnp.int32),
+            pltpu.VMEM((tiles, depths, 1, slab), jnp.int32),
+            pltpu.VMEM((2, tiles, 2, LANES, entries // 2), BF16),
+            pltpu.VMEM((2, tiles, 2, 1, entries // 2), jnp.int32),
+            pltpu.VMEM((lines, LANES), F32),
+            pltpu.VMEM((lines, LANES), F32),
+            dma((2,)),
             pltpu.VMEM((lines, LANES), F32),
             pltpu.VMEM((lines, 2 * LANES), BF16),
             pltpu.VMEM((lines, LANES), BF16),
-            pltpu.VMEM((tiles,) + block, F32),
-            pltpu.VMEM((tiles,) + block, F32),
+            pltpu.VMEM((tiles, 2) + block, F32),
+            pltpu.VMEM((tiles, 2) + block, F32),
             dma((tiles, depths)),
             dma((tiles, depths)),
-            dma((tiles,)),
-            dma((tiles,)),
+            dma((tiles, 2)),
+            dma((tiles, 2)),
             pltpu.VMEM((entries, pixels), F32),
             pltpu.VMEM((entries, pixels), F32),
             pltpu.VMEM((entries, pixels), F32),
@@ -554,24 +646,19 @@
             pltpu.VMEM((LANES, pixels), BF16),
             pltpu.VMEM((LANES, pixels), BF16),
             pltpu.VMEM((entries, LANES), F32),
-            pltpu.VMEM(block, F32),
+            pltpu.VMEM((2, 2) + slip, F32),
             pltpu.VMEM((3, pixels), F32),
             pltpu.VMEM((depths, 3, pixels), F32),
-            pltpu.VMEM((tiles,) + block, F32),
-            pltpu.VMEM((lines, LANES), F32),
-            pltpu.VMEM((lines // 2, LANES), F32),
+            pltpu.VMEM((tiles, 2, 2) + slip, F32),
             pltpu.VMEM((lines // 2, LANES), F32),
             pltpu.VMEM((depths, lines // 2, LANES), F32),
             pltpu.VMEM((lines, LANES), F32),
-            dma((tiles,)),
-            dma((tiles,)),
+            dma((tiles, 2, 2)),
+            dma((tiles, 2, 2)),
             dma((depths,)),
             dma((depths,)),
-            dma((2,)),
-            dma((2,)),
             dma((depths,)),
             dma((depths,)),
-            dma((2,)),
             dma((2,)),
         ],
         name="step",

time: 36.4 us -> 34.2 us (0.940)
  Pallas kernels: 35.6 us -> 33.4 us
    pallas_call x1, Pallas kernels: 34.8 us -> 32.6 us  [body(): pl.pallas_call(functools.partial(step_kernel, tiles, depths), out_shape=[...]
where the time goes in v3:
time: 34.2 us; the launch traced here: 34 us
  Pallas kernels  33.4 us (98%)
  between operations  0.64 us (2%)
    pallas_call x1, Pallas kernels, body(): pl.pallas_call(functools.partial(step_kernel, tiles, depths), out_shape=[...  32.6 us
    pallas_call x1, Pallas kernels, body(): pl.pallas_call(finish_kernel, out_shape=[jax.ShapeDtypeStruct(shape, F32)...  0.8 us

profile of v3, /device:TPU:0, one launch (start us, length us, event | category | flops | bytes accessed | tf_op | source)
XLA Modules:
  0.0 34.0 jit_solution(1369999785151524185)
XLA Ops:
  0.6 32.6 %step.1 = (f32[3,4,1024]{2,1,0:T(4,128)S(1)}, f32[10,2048]{1,0:T(8,128)S(1)}, f32[10,2048]{1,0:T(8,128)S(1)}, f32[10,2048]{1,0:T(8,128)S(1)}) custom-call(s32[4,1,128]{2,1,0:T(1,128)} %bitcast.5, s32[4,128]{1,0:T(4,128)} %bitcast.6, f32[3,2048]{1,0:T(4,128)} %place_in.1, f32[3,2048]{1,0:T(4,128)} %scale_in.1, f32[1,2048]{1,0:T(1,128)} %logit_in.1, ...), custom_call_target="tpu_custom_call" | custom-call | tf_op jit(solution)/shard_map/step/pallas_call | solution.py:614
  33.2 0.8 %finish.1 = (f32[3,4,1024]{2,1,0:T(4,128)}, f32[10,2048]{1,0:T(8,128)}, f32[10,2048]{1,0:T(8,128)}, f32[10,2048]{1,0:T(8,128)}) custom-call(f32[3,4,1024]{2,1,0:T(4,128)S(1)} %get-tuple-element.12.refs_0_, f32[10,2048]{1,0:T(8,128)S(1)} %get-tuple-element.13.refs_1_, f32[10,2048]{1,0:T(8,128)S(1)} %get-tuple-element.14.refs_2_, ...), custom_call_target="tpu_custom_call" | custom-call | tf_op jit(solution)/shard_map/finish/pallas_call | solution.py:669

commit v4 on v3

--- a/solution.py
+++ b/solution.py
@@ -15,7 +15,7 @@
 LOG2E = 1.4426950408889634
 PRODUCTS = ((0, 0), (0, 1), (1, 0), (0, 2), (1, 1), (2, 0))
 PULL_ROW, PULL_ROWS = 32, 32
-UNROLL = 16
+AHEAD, BACK = 8, 32
 
 
 def greet(peers):
@@ -233,17 +233,26 @@
             serve(*range(step, min(step + 2, tiles)))
     else:
         each_tile(serve)
-    each_tile(lambda step: back(step, 1).start())
+    if small:
+        for step in range(tiles - 1, 0, -1):
+            back(step, 1).start()
+    else:
+        each_tile(lambda step: back(step, 1).start())
     twin = remote(lists_ref, twin_ref, twin_sem.at[0], twin_sem.at[1], along(1))
     twin.start()
     for a, b in steps:
         asked(a, b).wait_send()
     for copy in copies[6:]:
         copy.wait()
-    for h in range(highs):
-        spaced = pl.ds(h, 10, stride=highs)
-        first_lines[spaced, :] = first_ref[:, h * LANES : (h + 1) * LANES]
-        second_lines[spaced, :] = second_ref[:, h * LANES : (h + 1) * LANES]
+    folds = [
+        (slice(p, min(p + 8, 10)), slice(h * LANES, (h + 1) * LANES),
+         pl.ds(p * highs + h, min(p + 8, 10) - p, stride=highs))
+        for h in range(highs)
+        for p in (0, 8)
+    ]
+    for top, part, spaced in folds:
+        first_lines[spaced, :] = first_ref[top, part]
+        second_lines[spaced, :] = second_ref[top, part]
     twin.wait()
 
     def note_twin(step):
@@ -359,7 +368,7 @@
     for part in range(2):
         screens.append(project(part))
         carried = lax.fori_loop(
-            part * (groups // 2), (part + 1) * (groups // 2), forward, carried, unroll=UNROLL
+            part * (groups // 2), (part + 1) * (groups // 2), forward, carried, unroll=AHEAD
         )
     trans, color = carried
 
@@ -453,7 +462,7 @@
         top = (part + 1) * (groups // 2)
         behinds = lax.fori_loop(
             0, groups // 2, lambda i, behind: backward(top - 1 - i, behind, part), behinds,
-            unroll=UNROLL,
+            unroll=BACK,
         )
         variance, center_x, center_y, conic_a, conic_b, conic_c, opacity = screens[part]
         flat = sums[part * span : (part + 1) * span, :].T
@@ -511,17 +520,25 @@
                 )
         return total
 
+    def gather(part, group):
+        for step in group:
+            for other in (0, 1) if not isinstance(step, int) or step else (1,):
+                grads(step, other, part).wait()
+        total = partial[...]
+        for step in group:
+            near = inbox[step, 0, part] if not isinstance(step, int) or step else grad_ref[part, core]
+            total = total + placed([near, inbox[step, 1, part]], step, part)
+        partial[...] = total
+
     partial[...] = jnp.zeros(partial.shape, F32)
     for part in (1, 0):
-        grads(0, 1, part).wait()
-        partial[...] += placed([grad_ref[part, core], inbox[0, 1, part]], 0, part)
-
-        def add(step):
-            for other in (0, 1):
-                grads(step, other, part).wait()
-            partial[...] += placed([inbox[step, 0, part], inbox[step, 1, part]], step, part)
-
-        each_tile(add)
+        if small:
+            take_at_once = 4 if part else 2
+            for step in range(0, tiles, take_at_once):
+                gather(part, range(step, min(step + take_at_once, tiles)))
+        else:
+            gather(part, [0])
+            each_tile(lambda step: gather(part, [step]))
 
     def side(index):
         return pl.ds(pl.multiple_of(index * size, 8), size)
@@ -559,12 +576,10 @@
             picture_ref[k, d : d + 1, :] = images_ref[d, k : k + 1, :]
     share.wait()
     finish(side(1 - core))
-    for h in range(highs):
-        part = slice(h * LANES, (h + 1) * LANES)
-        spaced = pl.ds(h, 10, stride=highs)
-        new_param_ref[:, part] = param_ref[spaced, :]
-        new_first_ref[:, part] = first_lines[spaced, :]
-        new_second_ref[:, part] = second_lines[spaced, :]
+    for top, part, spaced in folds:
+        new_param_ref[top, part] = param_ref[spaced, :]
+        new_first_ref[top, part] = first_lines[spaced, :]
+        new_second_ref[top, part] = second_lines[spaced, :]
 
 
 def adam_update(param, first, second, gradient):

time: 34.2 us -> 33.9 us (level)
  no operation moved by 1% of the time
where the time goes in v4:
time: 33.9 us; the launch traced here: 33.7 us
  Pallas kernels  33.1 us (98%)
  between operations  0.64 us (2%)
    pallas_call x1, Pallas kernels, body(): pl.pallas_call(functools.partial(step_kernel, tiles, depths), out_shape=[...  32.3 us
    pallas_call x1, Pallas kernels, body(): pl.pallas_call(finish_kernel, out_shape=[jax.ShapeDtypeStruct(shape, F32)...  0.8 us

profile of v4, /device:TPU:0, one launch (start us, length us, event | category | flops | bytes accessed | tf_op | source)
XLA Modules:
  0.0 33.7 jit_solution(18170723508545064758)
XLA Ops:
  0.6 32.3 %step.1 = (f32[3,4,1024]{2,1,0:T(4,128)S(1)}, f32[10,2048]{1,0:T(8,128)S(1)}, f32[10,2048]{1,0:T(8,128)S(1)}, f32[10,2048]{1,0:T(8,128)S(1)}) custom-call(s32[4,1,128]{2,1,0:T(1,128)} %bitcast.5, s32[4,128]{1,0:T(4,128)} %bitcast.6, f32[3,2048]{1,0:T(4,128)} %place_in.1, f32[3,2048]{1,0:T(4,128)} %scale_in.1, f32[1,2048]{1,0:T(1,128)} %logit_in.1, ...), custom_call_target="tpu_custom_call" | custom-call | tf_op jit(solution)/shard_map/step/pallas_call | solution.py:629
  33.0 0.8 %finish.1 = (f32[3,4,1024]{2,1,0:T(4,128)}, f32[10,2048]{1,0:T(8,128)}, f32[10,2048]{1,0:T(8,128)}, f32[10,2048]{1,0:T(8,128)}) custom-call(f32[3,4,1024]{2,1,0:T(4,128)S(1)} %get-tuple-element.12.refs_0_, f32[10,2048]{1,0:T(8,128)S(1)} %get-tuple-element.13.refs_1_, f32[10,2048]{1,0:T(8,128)S(1)} %get-tuple-element.14.refs_2_, ...), custom_call_target="tpu_custom_call" | custom-call | tf_op jit(solution)/shard_map/finish/pallas_call | solution.py:684

commit v5 on v4

--- a/solution.py
+++ b/solution.py
@@ -15,7 +15,7 @@
 LOG2E = 1.4426950408889634
 PRODUCTS = ((0, 0), (0, 1), (1, 0), (0, 2), (1, 1), (2, 0))
 PULL_ROW, PULL_ROWS = 32, 32
-AHEAD, BACK = 8, 32
+AHEAD, BACK = 16, 32
 
 
 def greet(peers):
@@ -103,8 +103,6 @@
             lax.fori_loop(1, tiles, one, 0)
 
     barrier = pltpu.get_barrier_semaphore()
-    for a, b in steps:
-        pl.semaphore_signal(barrier, inc=1, device_id=to(a, b), device_id_type=MESH)
     pairs = [
         (owner_in, owner_ref), (row_in, row_ref), (place_in, place_ref), (scale_in, scale_ref),
         (logit_in, logit_ref), (color_in, color_ref), (view_in, view_ref), (length_in, length_ref),
@@ -115,7 +113,11 @@
         pltpu.make_async_copy(source, target, loads.at[i])
         for i, (source, target) in enumerate(pairs)
     ]
-    for copy in copies:
+    for copy in copies[:2]:
+        copy.start()
+    for a, b in steps:
+        pl.semaphore_signal(barrier, inc=1, device_id=to(a, b), device_id_type=MESH)
+    for copy in copies[2:]:
         copy.start()
     miss_ref[...] = jnp.zeros(miss_ref.shape, BF16)
     spot = lax.broadcasted_iota(jnp.int32, (1, pixels), 1)

time: 33.9 us -> 33.8 us (level)
  no operation moved by 1% of the time
where the time goes in v5:
time: 33.8 us; the launch traced here: 33.7 us
  Pallas kernels  33 us (98%)
  between operations  0.64 us (2%)
    pallas_call x1, Pallas kernels, body(): pl.pallas_call(functools.partial(step_kernel, tiles, depths), out_shape=[...  32.2 us
    pallas_call x1, Pallas kernels, body(): pl.pallas_call(finish_kernel, out_shape=[jax.ShapeDtypeStruct(shape, F32)...  0.8 us

profile of v5, /device:TPU:0, one launch (start us, length us, event | category | flops | bytes accessed | tf_op | source)
XLA Modules:
  0.0 33.7 jit_solution(18113579363111760914)
XLA Ops:
  0.6 32.2 %step.1 = (f32[3,4,1024]{2,1,0:T(4,128)S(1)}, f32[10,2048]{1,0:T(8,128)S(1)}, f32[10,2048]{1,0:T(8,128)S(1)}, f32[10,2048]{1,0:T(8,128)S(1)}) custom-call(s32[4,1,128]{2,1,0:T(1,128)} %bitcast.5, s32[4,128]{1,0:T(4,128)} %bitcast.6, f32[3,2048]{1,0:T(4,128)} %place_in.1, f32[3,2048]{1,0:T(4,128)} %scale_in.1, f32[1,2048]{1,0:T(1,128)} %logit_in.1, ...), custom_call_target="tpu_custom_call" | custom-call | tf_op jit(solution)/shard_map/step/pallas_call | solution.py:631
  32.9 0.8 %finish.1 = (f32[3,4,1024]{2,1,0:T(4,128)}, f32[10,2048]{1,0:T(8,128)}, f32[10,2048]{1,0:T(8,128)}, f32[10,2048]{1,0:T(8,128)}) custom-call(f32[3,4,1024]{2,1,0:T(4,128)S(1)} %get-tuple-element.12.refs_0_, f32[10,2048]{1,0:T(8,128)S(1)} %get-tuple-element.13.refs_1_, f32[10,2048]{1,0:T(8,128)S(1)} %get-tuple-element.14.refs_2_, ...), custom_call_target="tpu_custom_call" | custom-call | tf_op jit(solution)/shard_map/finish/pallas_call | solution.py:686
